TPU v7x, 32 devices: a whole 2x2x4 slice. The times are simulated.
32 devices in a mesh: fsdp: 32 (over z, y, x, core).
Axes of the slice: x: 2, y: 2, z: 4, core: 2. Of those that a mesh axis runs over, the one named last changes fastest.
Arguments:
- act_in: bfloat16 [512, 196, 512], P('fsdp')
- labels: int32 [512], P('fsdp')
- layer_p: float32 [2, 2203648], P(None, 'fsdp')
- head_w: float32 [512, 1000], P('fsdp')
- small_p: float32 [4096], P('fsdp')
- layer_m: float32 [2, 2203648], P(None, 'fsdp')
- head_m: float32 [512, 1000], P('fsdp')
- small_m: float32 [4096], P('fsdp')
- layer_v: float32 [2, 2203648], P(None, 'fsdp')
- head_v: float32 [512, 1000], P('fsdp')
- small_v: float32 [4096], P('fsdp')
Outputs:
- output 1: float32 [], replicated
- output 2: float32 [2, 2203648], P(None, 'fsdp')
- output 3: float32 [512, 1000], P('fsdp')
- output 4: float32 [4096], P('fsdp')
- output 5: float32 [2, 2203648], P(None, 'fsdp')
- output 6: float32 [512, 1000], P('fsdp')
- output 7: float32 [4096], P('fsdp')
- output 8: float32 [2, 2203648], P(None, 'fsdp')
- output 9: float32 [512, 1000], P('fsdp')
- output 10: float32 [4096], P('fsdp')
All inputs are finite; a program needn't handle non-finite values.
Results may differ from a plain program's by a relative error of at most 0.00106585.
Values are sent between devices in bfloat16 or wider.
A program may use at most 1 GiB of HBM per device.

v0:
```python
import math
import jax
import jax.numpy as jnp
from jax import lax
from jax.experimental import pallas as pl
from jax.experimental.pallas import tpu as pltpu
from jax.sharding import PartitionSpec as P

LN_EPS = 1e-6
LEARN_RATE = 0.003
BETA_ONE = 0.9
BETA_TWO = 0.999
ADAM_EPS = 1e-8
WEIGHT_DECAY = 0.03
ADAM_STEP = 10
AXIS = 'fsdp'
GROUP = 32
ROWS = 8
LANES = 128
TILE = ROWS * LANES
HEAD_PAD = 1024

def row_offset(share_rows):
    return (lax.axis_index(AXIS) * share_rows) % ROWS


def share_to_window(share):
    share_rows = share.shape[0] // LANES
    num_tiles = -(-(share_rows + ROWS - 2) // ROWS)
    window = jnp.zeros((num_tiles * ROWS, LANES), share.dtype)
    window = lax.dynamic_update_slice(window, share.reshape(share_rows, LANES), (row_offset(share_rows), 0))
    return window.reshape(num_tiles, ROWS, LANES)


def window_to_share(window, share_len):
    share_rows = share_len // LANES
    rows = window.reshape(-1, LANES)
    return lax.dynamic_slice(rows, (row_offset(share_rows), 0), (share_rows, LANES)).reshape(share_len)


def piece_shapes(num_tokens, num_chans):
    tok_hid = num_chans // 2
    ch_hid = 4 * num_chans
    return [(num_tokens, tok_hid), (tok_hid, num_tokens), (num_chans, ch_hid), (ch_hid, num_chans), (num_chans,), (num_chans,), (tok_hid,), (num_tokens,), (num_chans,), (num_chans,), (ch_hid,), (num_chans,)]


def unpack_tiles(tiles, num_tokens, num_chans):
    pieces = []
    start = 0
    shapes = piece_shapes(num_tokens, num_chans)
    for shape_one in shapes[:4]:
        count = math.prod(shape_one) // TILE
        pieces.append(tiles[start:start + count].reshape(shape_one))
        start = start + count
    flat = tiles[start:].reshape(-1)
    start = 0
    for shape_one in shapes[4:]:
        pieces.append(flat[start:start + shape_one[0]])
        start = start + shape_one[0]
    return pieces


def pack_tiles(grads, flat_len):
    pieces = [grad.reshape(-1, ROWS, LANES) for grad in grads[:4]]
    used = sum(piece.shape[0] for piece in pieces) * TILE
    vectors = jnp.concatenate(grads[4:])
    vectors = jnp.pad(vectors, (0, flat_len - used - vectors.shape[0]))
    pieces.append(vectors.reshape(-1, ROWS, LANES))
    return jnp.concatenate(pieces, axis=0)


def head_to_tiles(head):
    rows = head.shape[0]
    head = jnp.pad(head, ((0, 0), (0, HEAD_PAD - head.shape[1])))
    return head.reshape(rows // ROWS, ROWS, HEAD_PAD // LANES, LANES).transpose(0, 2, 1, 3).reshape(-1, ROWS, LANES)


def tiles_to_head(tiles, rows):
    tiles = tiles.reshape(rows // ROWS, HEAD_PAD // LANES, ROWS, LANES)
    return tiles.transpose(0, 2, 1, 3).reshape(rows, HEAD_PAD)


MASK_CORE, MASK_X, MASK_Y, MASK_Z = 1, 2, 4, 8
PARTNERS = (MASK_CORE, MASK_X, MASK_Y, MASK_Z, 2 * MASK_Z, 3 * MASK_Z)
PERIOD = 4


class Peers:
    def __init__(self, me):
        self.bits = []
        for bit in range(5):
            val = lax.rem(lax.div(me, 1 << bit), 2)
            self.bits.append((val, 1 - val))
        self.known = {}

    def split(self, rel):
        if rel not in self.known:
            vals = [self.bits[bit][(rel >> bit) & 1] for bit in range(5)]
            pos = vals[0] + 2 * vals[1]
            group = vals[2] + 2 * vals[3] + 4 * vals[4]
            self.known[rel] = (group * PERIOD + pos, group, pos)
        return self.known[rel]

    def device(self, rel):
        return self.split(rel)[0]


def meet_partners(peers):
    barrier = pltpu.get_barrier_semaphore()
    for mask in PARTNERS:
        pl.semaphore_signal(barrier, inc=1, device_id=(peers.device(mask),), device_id_type=pl.DeviceIdType.MESH)
    pl.semaphore_wait(barrier, len(PARTNERS))


def gather_kernel(inner0_ref, inner1_ref, misc_ref, flat0_ref, flat1_ref, extra_ref, misc_all, bound, local_sems, send_sems, recv_sems):
    peers = Peers(lax.axis_index(AXIS))
    inner = inner0_ref.shape[0]
    stride = inner + 1
    own_refs = (inner0_ref, inner1_ref, misc_ref)
    colours = ((MASK_Y, MASK_X), (MASK_X, MASK_Y), (MASK_X, MASK_Y))

    def place(arr, rel):
        dev, group, pos = peers.split(rel)
        if arr == 2:
            return misc_all.at[dev]
        flat = (flat0_ref, flat1_ref)[arr]
        return flat.at[group, pl.ds(stride * pos + 1, inner)]

    own_copies = [pltpu.make_async_copy(own_refs[arr], place(arr, 0), local_sems.at[arr]) for arr in range(3)]
    for copy in own_copies:
        copy.start()
    meet_partners(peers)
    sends = []

    def send(arr, rel, mask):
        here = place(arr, rel)
        copy = pltpu.make_async_remote_copy(
            src_ref=own_refs[arr] if rel == 0 else here, dst_ref=here,
            send_sem=send_sems.at[arr, rel ^ mask], recv_sem=recv_sems.at[arr, rel ^ mask],
            device_id=(peers.device(mask),), device_id_type=pl.DeviceIdType.MESH)
        copy.start()
        sends.append(copy)

    def receive(arr, rel):
        here = place(arr, rel)
        pltpu.make_async_remote_copy(
            src_ref=here, dst_ref=here, send_sem=send_sems.at[arr, rel], recv_sem=recv_sems.at[arr, rel],
            device_id=(peers.device(0),), device_id_type=pl.DeviceIdType.MESH).wait_recv()

    for mask_pos in range(6):
        for arr in range(3):
            first, second = colours[arr]
            send(arr, 0, (MASK_Z, first, second, 2 * MASK_Z, 3 * MASK_Z, MASK_CORE)[mask_pos])
    for dist, use_first, use_second in ((0, 1, 0), (1, 0, 0), (0, 0, 1), (1, 1, 0), (0, 1, 1), (2, 0, 0), (1, 0, 1), (2, 1, 0),
                                        (1, 1, 1), (3, 0, 0), (2, 0, 1), (3, 1, 0), (2, 1, 1), (3, 0, 1), (3, 1, 1)):
        for arr in range(3):
            first, second = colours[arr]
            rel = dist * MASK_Z + use_first * first + use_second * second
            receive(arr, rel)
            if not use_second:
                if not use_first:
                    send(arr, rel, first)
                send(arr, rel, second)
            send(arr, rel, MASK_CORE)
    for rel in range(MASK_CORE, GROUP, 2):
        for arr in range(3):
            receive(arr, rel)
    for copy in own_copies:
        copy.wait()
    for copy in sends:
        copy.wait_send()

    for layer_idx in range(2):
        for group in range(GROUP // PERIOD):
            for pos in range(PERIOD + 1):
                tile = None
                if pos < PERIOD:
                    tile = misc_all[group * PERIOD + pos, 2 * layer_idx]
                if pos > 0:
                    left = misc_all[group * PERIOD + pos - 1, 2 * layer_idx + 1]
                    tile = left if tile is None else tile + left
                bound[layer_idx, pos, group, 0] = tile
    extra_ref[...] = misc_all[:, 4:]
    edges = []
    for layer_idx in range(2):
        flat = (flat0_ref, flat1_ref)[layer_idx]
        for pos in range(PERIOD + 1):
            edges.append(pltpu.make_async_copy(bound.at[layer_idx, pos], flat.at[:, pl.ds(stride * pos, 1)], local_sems.at[3 + layer_idx * (PERIOD + 1) + pos]))
    for copy in edges:
        copy.start()
    for copy in edges:
        copy.wait()


def gather_shares(window0, window1, extra):
    num_tiles = window0.shape[0]
    num_extra = extra.shape[0]
    inner = num_tiles - 2
    misc = jnp.concatenate([window0[:1], window0[-1:], window1[:1], window1[-1:], extra], axis=0)
    flat = (GROUP // PERIOD, PERIOD * (num_tiles - 1) + 1, ROWS, LANES)
    vmem = pl.BlockSpec(memory_space=pltpu.VMEM)
    hbm = pl.BlockSpec(memory_space=pl.ANY)
    dtype = window0.dtype
    return pl.pallas_call(
        gather_kernel,
        out_shape=(jax.ShapeDtypeStruct(flat, dtype), jax.ShapeDtypeStruct(flat, dtype), jax.ShapeDtypeStruct((GROUP, num_extra, ROWS, LANES), dtype)),
        in_specs=[vmem] * 3,
        out_specs=(hbm, hbm, vmem),
        scratch_shapes=[
            pltpu.VMEM((GROUP, num_extra + 4, ROWS, LANES), dtype),
            pltpu.VMEM((2, PERIOD + 1, GROUP // PERIOD, 1, ROWS, LANES), dtype),
            pltpu.SemaphoreType.DMA((3 + 2 * (PERIOD + 1),)),
            pltpu.SemaphoreType.DMA((3, GROUP)),
            pltpu.SemaphoreType.DMA((3, GROUP)),
        ],
        compiler_params=pltpu.CompilerParams(collective_id=1, has_side_effects=True),
        name='gather_shares',
    )(window0[1:-1], window1[1:-1], misc)


def scatter_kernel(grad0_ref, grad1_ref, extra_ref, out0_ref, out1_ref, own0, own1, core0, core1, first0, first1, second0, second1, far0, far1,
                   load_sems, send_sems, core_sems, first_sems, second_sems, far_sems):
    peers = Peers(lax.axis_index(AXIS))
    num_tiles = out0_ref.shape[0]
    num_extra = extra_ref.shape[1]
    own, near, first_in, second_in, far_in = (own0, own1), (core0, core1), (first0, first1), (second0, second1), (far0, far1)
    colours = ((MASK_X, MASK_Y), (MASK_Y, MASK_X))
    dists = (3, 2, 1, 0)
    sends = []

    def source(part, rel):
        dev, group, pos = peers.split(rel)
        if part == 2:
            return extra_ref.at[dev]
        grad = (grad0_ref, grad1_ref)[part]
        return grad.at[group, pl.ds((num_tiles - 1) * pos, num_tiles)]

    def slot(part, buffers, pos):
        if part == 2:
            return buffers[1].at[pos, pl.ds(num_tiles, num_extra)]
        return buffers[part].at[pos, pl.ds(0, num_tiles)]

    def post(src, dst, send_sem, recv_sem, mask):
        copy = pltpu.make_async_remote_copy(src_ref=src, dst_ref=dst, send_sem=send_sem, recv_sem=recv_sem,
                                            device_id=(peers.device(mask),), device_id_type=pl.DeviceIdType.MESH)
        copy.start()
        sends.append(copy)

    def expect(dst, send_sem, recv_sem):
        pltpu.make_async_remote_copy(src_ref=dst, dst_ref=dst, send_sem=send_sem, recv_sem=recv_sem,
                                     device_id=(peers.device(0),), device_id_type=pl.DeviceIdType.MESH).wait_recv()

    def targets(dist):
        return [(dist * 4 + pos, dist * MASK_Z + pos * MASK_X) for pos in (3, 2, 1, 0)]

    loads = {}
    for dist in dists:
        for pos, rel in targets(dist):
            for part in range(3):
                loads[part, pos] = pltpu.make_async_copy(source(part, rel), slot(part, own, pos), load_sems.at[part, pos])
                loads[part, pos].start()
    meet_partners(peers)
    for dist in dists:
        for pos, rel in targets(dist):
            for part in range(3):
                post(source(part, rel | MASK_CORE), slot(part, near, pos), send_sems.at[part, pos], core_sems.at[part, pos], MASK_CORE)

    def fold_core(dist):
        for pos, rel in targets(dist):
            for part in range(3):
                loads[part, pos].wait()
                expect(slot(part, near, pos), send_sems.at[part, pos], core_sems.at[part, pos])
            for side in range(2):
                own[side][pos] += near[side][pos]
        for side in range(2):
            mask, other = colours[side]
            for which in (1, 0):
                pos = dist * 4 + (mask + which * other) // MASK_X
                index = dist * 2 + which
                post(own[side].at[pos], first_in[side].at[index], send_sems.at[3 + side, index], first_sems.at[side, index], mask)

    def fold_first(dist):
        for side in range(2):
            mask, other = colours[side]
            for which in (1, 0):
                pos = dist * 4 + which * other // MASK_X
                index = dist * 2 + which
                expect(first_in[side].at[index], send_sems.at[3 + side, index], first_sems.at[side, index])
                own[side][pos] += first_in[side][index]
        for side in range(2):
            mask, other = colours[side]
            post(own[side].at[dist * 4 + other // MASK_X], second_in[side].at[dist], send_sems.at[3 + side, 8 + dist], second_sems.at[side, dist], other)

    def fold_second(dist):
        for side in range(2):
            expect(second_in[side].at[dist], send_sems.at[3 + side, 8 + dist], second_sems.at[side, dist])
            own[side][dist * 4] += second_in[side][dist]
        if dist:
            for side in range(2):
                post(own[side].at[dist * 4], far_in[side].at[dist - 1], send_sems.at[3 + side, 12 + dist], far_sems.at[side, dist - 1], dist * MASK_Z)

    for dist in dists:
        fold_core(dist)
    fold_first(3)
    fold_first(2)
    fold_second(3)
    fold_first(1)
    fold_second(2)
    fold_first(0)
    fold_second(1)
    fold_second(0)
    for side in range(2):
        total = own[side][0]
        for dist in (3, 2, 1):
            expect(far_in[side].at[dist - 1], send_sems.at[3 + side, 12 + dist], far_sems.at[side, dist - 1])
            total = total + far_in[side][dist - 1]
        (out0_ref, out1_ref)[side][...] = total
    for copy in sends:
        copy.wait_send()


def scatter_grads(grad0, grad1, extra, num_tiles):
    num_extra = extra.shape[1]
    sizes = (num_tiles, num_tiles + num_extra)
    vmem = pl.BlockSpec(memory_space=pltpu.VMEM)
    hbm = pl.BlockSpec(memory_space=pl.ANY)

    def buffers(count):
        return [pltpu.VMEM((count, size, ROWS, LANES), jnp.float32) for size in sizes]

    return pl.pallas_call(
        scatter_kernel,
        out_shape=tuple(jax.ShapeDtypeStruct((size, ROWS, LANES), jnp.float32) for size in sizes),
        in_specs=[hbm] * 3,
        out_specs=(vmem, vmem),
        scratch_shapes=buffers(16) + buffers(16) + buffers(8) + buffers(4) + buffers(3) + [
            pltpu.SemaphoreType.DMA((3, 16)),
            pltpu.SemaphoreType.DMA((5, 16)),
            pltpu.SemaphoreType.DMA((3, 16)),
            pltpu.SemaphoreType.DMA((2, 8)),
            pltpu.SemaphoreType.DMA((2, 4)),
            pltpu.SemaphoreType.DMA((2, 3)),
        ],
        compiler_params=pltpu.CompilerParams(collective_id=2, has_side_effects=True),
        name='scatter_grads',
    )(grad0, grad1, extra)


def sum_kernel(x_ref, out_ref, held, local_sem, send_sems, recv_sems):
    me = lax.axis_index(AXIS)
    barrier = pltpu.get_barrier_semaphore()
    for step in range(1, GROUP):
        pl.semaphore_signal(barrier, inc=1, device_id=((me + step) % GROUP,), device_id_type=pl.DeviceIdType.MESH)
    own = pltpu.make_async_copy(x_ref, held.at[me], local_sem)
    own.start()
    pl.semaphore_wait(barrier, GROUP - 1)
    sends = []
    for step in range(1, GROUP):
        copy = pltpu.make_async_remote_copy(
            src_ref=x_ref, dst_ref=held.at[me], send_sem=send_sems.at[step], recv_sem=recv_sems.at[me],
            device_id=((me + step) % GROUP,), device_id_type=pl.DeviceIdType.MESH)
        copy.start()
        sends.append(copy)
    own.wait()
    for step in range(1, GROUP):
        peer = (me + step) % GROUP
        pltpu.make_async_remote_copy(
            src_ref=x_ref, dst_ref=held.at[peer], send_sem=send_sems.at[step], recv_sem=recv_sems.at[peer],
            device_id=(peer,), device_id_type=pl.DeviceIdType.MESH).wait_recv()
    for copy in sends:
        copy.wait_send()
    out_ref[...] = jnp.sum(held[...], axis=0)


def sum_over_devices(values):
    block = jnp.zeros((ROWS, LANES), jnp.float32)
    for pos, value in enumerate(values):
        block = block.at[0, pos].set(value)
    total = pl.pallas_call(
        sum_kernel,
        out_shape=jax.ShapeDtypeStruct((ROWS, LANES), jnp.float32),
        in_specs=[pl.BlockSpec(memory_space=pltpu.VMEM)],
        out_specs=pl.BlockSpec(memory_space=pltpu.VMEM),
        scratch_shapes=[
            pltpu.VMEM((GROUP, ROWS, LANES), jnp.float32),
            pltpu.SemaphoreType.DMA,
            pltpu.SemaphoreType.DMA((GROUP,)),
            pltpu.SemaphoreType.DMA((GROUP,)),
        ],
        compiler_params=pltpu.CompilerParams(collective_id=0, has_side_effects=True),
        name='sum_over_devices',
    )(block)
    return [total[0, pos] for pos in range(len(values))]


def layer_norm(x_in, ln_gain, ln_shift):
    x_f = x_in.astype(jnp.float32)
    mean_val = jnp.mean(x_f, axis=-1, keepdims=True)
    var_val = jnp.mean(jnp.square(x_f - mean_val), axis=-1, keepdims=True)
    normed = (x_f - mean_val) * lax.rsqrt(var_val + LN_EPS)
    return (normed * ln_gain.astype(jnp.float32) + ln_shift.astype(jnp.float32)).astype(jnp.bfloat16)


def gelu_both(hidden):
    scale = math.sqrt(2.0 / math.pi)
    square = hidden * hidden
    tanh_val = jnp.tanh(hidden * (scale + (scale * 0.044715) * square))
    cdf = 0.5 + 0.5 * tanh_val
    slope = cdf + (0.5 * hidden) * (1.0 - tanh_val * tanh_val) * (scale + (3.0 * scale * 0.044715) * square)
    return (hidden * cdf).astype(jnp.bfloat16), slope


def norm_grad(x_in, ln_gain, ln_shift, d_normed):
    _, pullback = jax.vjp(layer_norm, x_in, ln_gain.astype(jnp.float32), ln_shift.astype(jnp.float32))
    d_x, d_gain, d_shift = pullback(d_normed.astype(jnp.bfloat16))
    return d_x.astype(jnp.float32), d_gain, d_shift


def scoped(tag, spec, lhs, rhs, **kwargs):
    with jax.named_scope(tag):
        return jnp.einsum(spec, lhs, rhs, **kwargs)


def layer_forward(x_in, weights, tag):
    w_tok1, w_tok2, w_ch1, w_ch2, ln1_g, ln1_b, b_tok1, b_tok2, ln2_g, ln2_b, b_ch1, b_ch2 = weights
    normed = layer_norm(x_in, ln1_g, ln1_b)
    hid_tok = scoped(tag + '_tok1', 'bsc,sj->bcj', normed, w_tok1, preferred_element_type=jnp.float32) + b_tok1.astype(jnp.float32)
    act_tok, slope_tok = gelu_both(hid_tok)
    with jax.named_scope(tag + '_tok2'):
        tok_out = jnp.einsum('bcj,js->bsc', act_tok, w_tok2, preferred_element_type=jnp.float32) + b_tok2.astype(jnp.float32)[:, None]
        after_tok = (x_in.astype(jnp.float32) + tok_out).astype(jnp.bfloat16)
    normed2 = layer_norm(after_tok, ln2_g, ln2_b)
    hid_ch = scoped(tag + '_ch1', 'bsc,cd->bsd', normed2, w_ch1, preferred_element_type=jnp.float32) + b_ch1.astype(jnp.float32)
    act_ch, slope_ch = gelu_both(hid_ch)
    with jax.named_scope(tag + '_ch2'):
        ch_out = jnp.einsum('bsd,dc->bsc', act_ch, w_ch2, preferred_element_type=jnp.float32) + b_ch2.astype(jnp.float32)
        layer_out = (after_tok.astype(jnp.float32) + ch_out).astype(jnp.bfloat16)
    return layer_out, (x_in, normed, slope_tok, act_tok, after_tok, normed2, slope_ch, act_ch)


def layer_backward(d_out, weights, cache, tag):
    w_tok1, w_tok2, w_ch1, w_ch2, ln1_g, ln1_b, b_tok1, b_tok2, ln2_g, ln2_b, b_ch1, b_ch2 = weights
    x_in, normed, slope_tok, act_tok, after_tok, normed2, slope_ch, act_ch = cache
    d_out_bf = d_out.astype(jnp.bfloat16)
    g_b_ch2 = jnp.sum(d_out, axis=(0, 1))
    g_w_ch2 = scoped(tag + '_gw2', 'bsd,bsc->dc', act_ch, d_out_bf, preferred_element_type=jnp.float32)
    with jax.named_scope(tag + '_dact'):
        d_act_ch = jnp.einsum('bsc,dc->bsd', d_out_bf, w_ch2, preferred_element_type=jnp.float32)
        d_hid_ch = d_act_ch.astype(jnp.bfloat16).astype(jnp.float32) * slope_ch
        d_hid_ch_bf = d_hid_ch.astype(jnp.bfloat16)
        g_b_ch1 = jnp.sum(d_hid_ch, axis=(0, 1))
    g_w_ch1 = scoped(tag + '_gw1', 'bsc,bsd->cd', normed2, d_hid_ch_bf, preferred_element_type=jnp.float32)
    d_normed2 = scoped(tag + '_dnorm2', 'bsd,cd->bsc', d_hid_ch_bf, w_ch1, preferred_element_type=jnp.float32)
    with jax.named_scope(tag + '_ln2'):
        d_after_ln, g_ln2_g, g_ln2_b = norm_grad(after_tok, ln2_g, ln2_b, d_normed2)
    d_after = d_after_ln + d_out
    d_after_bf = d_after.astype(jnp.bfloat16)
    g_b_tok2 = jnp.sum(d_after, axis=(0, 2))
    g_w_tok2 = scoped(tag + '_gt2', 'bcj,bsc->js', act_tok, d_after_bf, preferred_element_type=jnp.float32)
    with jax.named_scope(tag + '_dtok'):
        d_act_tok = jnp.einsum('bsc,js->bcj', d_after_bf, w_tok2, preferred_element_type=jnp.float32)
        d_hid_tok = d_act_tok.astype(jnp.bfloat16).astype(jnp.float32) * slope_tok
        d_hid_tok_bf = d_hid_tok.astype(jnp.bfloat16)
        g_b_tok1 = jnp.sum(d_hid_tok, axis=(0, 1))
    g_w_tok1 = scoped(tag + '_gt1', 'bsc,bcj->sj', normed, d_hid_tok_bf, preferred_element_type=jnp.float32)
    d_normed = scoped(tag + '_dnt', 'bcj,sj->bsc', d_hid_tok_bf, w_tok1, preferred_element_type=jnp.float32)
    d_in_ln, g_ln1_g, g_ln1_b = norm_grad(x_in, ln1_g, ln1_b, d_normed)
    d_in = d_in_ln + d_after
    return d_in, [g_w_tok1, g_w_tok2, g_w_ch1, g_w_ch2, g_ln1_g, g_ln1_b, g_b_tok1, g_b_tok2, g_ln2_g, g_ln2_b, g_b_ch1, g_b_ch2]


def head_step(hidden, labels, small_full, head_full, num_classes, global_b):
    num_tokens = hidden.shape[1]
    num_chans = hidden.shape[2]
    lnf_g = small_full[:num_chans]
    lnf_b = small_full[num_chans:2 * num_chans]
    head_b = small_full[2 * num_chans:2 * num_chans + num_classes]
    normed = layer_norm(hidden, lnf_g, lnf_b)
    pooled = (jnp.sum(normed, axis=1, dtype=jnp.float32) / num_tokens).astype(jnp.bfloat16)
    is_class = jnp.arange(HEAD_PAD)[None, :] < num_classes
    logits = jnp.dot(pooled, head_full, preferred_element_type=jnp.float32) + jnp.pad(head_b.astype(jnp.float32), (0, HEAD_PAD - num_classes))
    logits = jnp.where(is_class, logits, -jnp.inf)
    log_norm = jax.nn.logsumexp(logits, axis=-1)
    is_label = jnp.arange(HEAD_PAD)[None, :] == labels[:, None]
    picked = jnp.sum(jnp.where(is_label, logits, 0.0), axis=-1)
    loss_sum = jnp.sum(log_norm - picked)
    d_logits = (jnp.exp(logits - log_norm[:, None]) - is_label.astype(jnp.float32)) / global_b
    d_logits_bf = d_logits.astype(jnp.bfloat16)
    g_head_b = jnp.sum(d_logits, axis=0)[:num_classes]
    g_head_w = jnp.einsum('bc,bk->ck', pooled, d_logits_bf, preferred_element_type=jnp.float32)
    d_pooled = jnp.einsum('bk,ck->bc', d_logits_bf, head_full, preferred_element_type=jnp.float32)
    d_normed = jnp.broadcast_to((d_pooled / num_tokens)[:, None, :], normed.shape)
    d_hidden, g_lnf_g, g_lnf_b = norm_grad(hidden, lnf_g, lnf_b, d_normed)
    g_small = jnp.concatenate([g_lnf_g, g_lnf_b, g_head_b])
    return loss_sum, d_hidden, g_head_w, g_small


def adam_update(master, gradient, moment, second, decay_rate):
    moment_new = BETA_ONE * moment + (1.0 - BETA_ONE) * gradient
    second_new = BETA_TWO * second + (1.0 - BETA_TWO) * gradient * gradient
    m_hat = moment_new / (1.0 - BETA_ONE ** ADAM_STEP)
    v_hat = second_new / (1.0 - BETA_TWO ** ADAM_STEP)
    master_new = master - LEARN_RATE * (m_hat / (jnp.sqrt(v_hat) + ADAM_EPS) + decay_rate * master)
    return master_new, moment_new, second_new


def solution(mesh):
    row_spec = P(AXIS)
    layer_spec = P(None, AXIS)
    in_specs = (row_spec, row_spec, layer_spec, row_spec, row_spec, layer_spec, row_spec, row_spec, layer_spec, row_spec, row_spec)
    out_specs = (P(),) + in_specs[2:]

    def device_step(act_in, labels, layer_p, head_w, small_p, layer_m, head_m, small_m, layer_v, head_v, small_v):
        local_b, num_tokens, num_chans = act_in.shape
        global_b = local_b * GROUP
        num_layers, share_len = layer_p.shape
        flat_len = share_len * GROUP
        head_rows, num_classes = head_w.shape
        small_len = small_p.shape[0]
        mat_len = 2 * num_tokens * (num_chans // 2) + 8 * num_chans * num_chans

        windows = [share_to_window(layer_p[layer_idx].astype(jnp.bfloat16)) for layer_idx in range(num_layers)]
        win_tiles = windows[0].shape[0]
        head_tiles = head_to_tiles(head_w.astype(jnp.bfloat16))
        small_tile = jnp.pad(small_p.astype(jnp.bfloat16).reshape(1, 1, small_len), ((0, 0), (0, ROWS - 1), (0, 0)))
        num_head = head_tiles.shape[0]
        flat0, flat1, extra = gather_shares(windows[0], windows[1], jnp.concatenate([head_tiles, small_tile], axis=0))

        weights = []
        caches = []
        hidden = act_in
        for layer_idx, flat in enumerate((flat0, flat1)):
            weights.append(unpack_tiles(flat.reshape(-1, ROWS, LANES), num_tokens, num_chans))
            hidden, cache = layer_forward(hidden, weights[layer_idx], f'f{layer_idx}')
            caches.append(cache)
        head_full = tiles_to_head(extra[:, :num_head], head_rows * GROUP)
        small_full = extra[:, num_head, 0].reshape(-1)
        loss_sum, d_hidden, g_head_w, g_small = head_step(hidden, labels, small_full, head_full, num_classes, global_b)

        head_blocks = head_to_tiles(g_head_w).reshape(GROUP, num_head, ROWS, LANES)
        g_small = jnp.pad(g_small, (0, small_len * GROUP - g_small.shape[0])).reshape(GROUP, 1, 1, small_len)
        small_blocks = jnp.pad(g_small, ((0, 0), (0, 0), (0, ROWS - 1), (0, 0)))
        packed = [None] * num_layers
        for layer_idx in reversed(range(num_layers)):
            d_hidden, grads = layer_backward(d_hidden, weights[layer_idx], caches[layer_idx], f'b{layer_idx}')
            packed[layer_idx] = pack_tiles(grads, flat_len).reshape(flat0.shape)
        summed0, summed1 = scatter_grads(packed[0], packed[1], jnp.concatenate([head_blocks, small_blocks], axis=1), win_tiles)
        layer_g = jnp.stack([window_to_share(summed0, share_len), window_to_share(summed1[:win_tiles], share_len)])
        head_g = tiles_to_head(summed1[win_tiles:win_tiles + num_head], head_rows)[:, :num_classes]
        small_g = summed1[win_tiles + num_head, 0]

        sq_local = jnp.sum(jnp.square(layer_g)) + jnp.sum(jnp.square(head_g)) + jnp.sum(jnp.square(small_g))
        loss_total, sq_total = sum_over_devices([loss_sum, sq_local])
        loss_value = loss_total / global_b
        clip_scale = 1.0 / jnp.maximum(1.0, jnp.sqrt(sq_total))
        flat_pos = lax.axis_index(AXIS) * share_len + jnp.arange(share_len)
        layer_decay = jnp.where(flat_pos < mat_len, WEIGHT_DECAY, 0.0)[None, :]
        new_lp, new_lm, new_lv = adam_update(layer_p, layer_g * clip_scale, layer_m, layer_v, layer_decay)
        new_hw, new_hm, new_hv = adam_update(head_w, head_g * clip_scale, head_m, head_v, WEIGHT_DECAY)
        new_sp, new_sm, new_sv = adam_update(small_p, small_g * clip_scale, small_m, small_v, 0.0)
        return (loss_value, new_lp, new_hw, new_sp, new_lm, new_hm, new_sm, new_lv, new_hv, new_sv)

    return jax.shard_map(device_step, mesh=mesh, in_specs=in_specs, out_specs=out_specs, check_vma=False)
```

profile of v0, /device:TPU:0, one launch (start us, length us, event | category | flops | bytes accessed | tf_op | source)
XLA Modules:
  0.0 647.3 jit_solution(2305131012770309244)
XLA Ops:
  2.6 5.3 convert_reduce_fusion.5
  17.3 55.1 %gather_shares.1 = (bf16[8,269,8,128]{3,2,1,0:T(8,128)(2,1)}, bf16[8,269,8,128]{3,2,1,0:T(8,128)(2,1)}, bf16[32,17,8,128]{3,2,1,0:T(8,128)(2,1)}) custom-call(bf16[66,8,128]{2,1,0:T(8,128)(2,1)} %slice_bitcast_fusion.2.inner0_ref, bf16[66,8,128]{2,1,0:T(8,128)(2,1)} %slice_bitcast_fusion.1.inner1_ref, bf16[21,8,128]{2,1,0:T(8,128)(2,1)} %copy-done.57), custom_call_target="tpu_custom_call" | custom-call | tf_op jit(solution)/shard_map/gather_shares/pallas_call | solution.py:204
  111.8 5.7 fusion.119
  117.7 6.3 convert_reduce_fusion.4
  126.8 12.5 %fusion.108 = f32[16,196,2048]{2,1,0:T(8,128)} fusion(bf16[512,2048,1]{1,0,2:T(8,128)(2,1)S(1)} %copy-done.17, bf16[16,196,512]{2,1,0:T(8,128)(2,1)S(1)} %get-tuple-element.103, f32[512]{0:T(512)S(1)} %copy-done.75, f32[512]{0:T(512)S(1)} %copy-done.60, f32[16,196]{1,0:T(8,128)S(1)} %fusion.149, f32[16,196]{1,0:T(8,128)S(1)} %broadcast_multiply_fusion.3), kind=kOutput, calls=%fused_computation.159 | convolution fusion | flops 6586302464 | bytes 31027712 | tf_op jit(solution)/shard_map/f0_ch1/bsc,cd->bsd/dot_general | solution.py:421
  139.3 16.5 %convert_reduce_fusion.3 = (f32[16,196]{1,0:T(8,128)S(1)}, bf16[16,196,512]{2,1,0:T(8,128)(2,1)S(1)}) fusion(f32[512]{0:T(512)S(1)} %copy-done.81, bf16[2048,512,1]{1,0,2:T(8,128)(2,1)} %reshape.462, f32[16,196,2048]{2,1,0:T(8,128)} %fusion.108, f32[2048]{0:T(1024)S(1)} %copy-done.64, bf16[16,196,512]{2,1,0:T(8,128)(2,1)S(1)} %get-tuple-element.103), kind=kOutput, calls=%fused_computation.27 | convolution fusion | flops 6644102144 | bytes 34232576 | tf_op jit(solution)/shard_map/f0_ch2/bsd,dc->bsc/dot_general | solution.py:436
  167.2 19.3 %multiply_convert_fusion = (bf16[16,196,2048]{2,1,0:T(8,128)(2,1)}, f32[16,196,2048]{2,1,0:T(8,128)}) fusion(f32[2048]{0:T(1024)S(1)} %copy-done.66, bf16[512,2048,1]{1,0,2:T(8,128)(2,1)} %reshape.465, bf16[16,196,512]{2,1,0:T(8,128)(2,1)S(1)} %get-tuple-element.107, f32[512]{0:T(512)S(1)} %copy-done.79, f32[512]{0:T(512)S(1)} %copy-done.62, ...), kind=kOutput, calls=%fused_computation.2 | convolution fusion | flops 6644105216 | bytes 43880960 | tf_op jit(solution)/shard_map/f1_ch1/bsc,cd->bsd/dot_general | solution.py:421
  186.5 11.5 %convert_reduce_fusion.9 = (f32[16,196]{1,0:T(8,128)S(1)}, bf16[16,196,512]{2,1,0:T(8,128)(2,1)S(1)}) fusion(f32[512]{0:T(512)S(1)} %copy-done.80, bf16[16,196,2048]{2,1,0:T(8,128)(2,1)} %get-tuple-element.108, bf16[2048,512,1]{1,0,2:T(8,128)(2,1)} %reshape.466, bf16[16,196,512]{2,1,0:T(8,128)(2,1)S(1)} %get-tuple-element.107), kind=kOutput, calls=%fused_computation.65 | convolution fusion | flops 6586299392 | bytes 21379328 | tf_op jit(solution)/shard_map/f1_ch2/bsd,dc->bsc/dot_general | solution.py:436
  208.4 24.1 %fusion.183 = (f32[2048]{0:T(1024)S(1)}, bf16[16,196,2048]{2,1,0:T(8,128)(2,1)}) fusion(f32[16,196,2048]{2,1,0:T(8,128)} %get-tuple-element.109, f32[2048]{0:T(1024)S(1)} %copy-done.66, bf16[2048,512,1]{1,0,2:T(8,128)(2,1)S(1)} %copy-done.19, bf16[16,196,512]{2,1,0:T(8,128)(2,1)S(1)} %get-tuple-element.111, f32[16,196]{1,0:T(8,128)S(1)} %add_multiply_fusion.7, ...), kind=kOutput, calls=%fused_computation.301 | convolution fusion | flops 6717962240 | bytes 43944960 | tf_op jit(solution)/shard_map/b1_dact/bsc,dc->bsd/dot_general | solution.py:448
  232.6 9.9 %convolution_bitcast_fusion = f32[2048,512]{1,0:T(8,128)} fusion(bf16[16,196,2048]{2,1,0:T(8,128)(2,1)S(1)} %bitcast.223, bf16[16,196,512]{2,1,0:T(8,128)(2,1)S(1)} %get-tuple-element.111, f32[16,196]{1,0:T(8,128)S(1)} %add_multiply_fusion.7, f32[16,196]{1,0:T(8,128)S(1)} %multiply_multiply_fusion.7, f32[16,512]{1,0:T(8,128)S(1)} %fusion.139, ...), kind=kOutput, calls=%fused_computation.145 | convolution fusion | flops 6589513728 | bytes 20335616 | tf_op jit(solution)/shard_map/b1_gw2/bsd,bsc->dc/dot_general | solution.py:421
  247.2 16.4 %fusion.75 = (f32[512]{0:T(512)S(1)}, f32[16,196]{1,0:T(8,128)S(1)}, f32[16,196]{1,0:T(8,128)S(1)}, f32[512]{0:T(512)S(1)}, bf16[16,196,512]{2,1,0:T(8,128)(2,1)}) fusion(bf16[16,196,512]{2,1,0:T(8,128)(2,1)} %copy-done, f32[16,196]{1,0:T(8,128)S(1)} %fusion.151, f32[16,196]{1,0:T(8,128)S(1)} %broadcast_multiply_fusion.1, f32[512]{0:T(512)S(1)} %copy-done.62, ...), kind=kOutput, calls=%fused_computation.125 | convolution fusion | flops 6597534720 | bytes 21421056 | tf_op jit(solution)/shard_map/b1_dnorm2/bsd,cd->bsc/dot_general | solution.py:421
  263.7 14.4 %fusion.89 = f32[512,2048]{1,0:T(8,128)} fusion(bf16[16,196,2048]{2,1,0:T(8,128)(2,1)} %get-tuple-element.126, bf16[16,196,512]{2,1,0:T(8,128)(2,1)S(1)} %copy-done.1, f32[512]{0:T(512)S(1)} %copy-done.79, f32[512]{0:T(512)S(1)} %copy-done.62, f32[16,196]{1,0:T(8,128)S(1)} %fusion.151, f32[16,196]{1,0:T(8,128)S(1)} %broadcast_multiply_fusion.1), kind=kOutput, calls=%fused_computation.143 | convolution fusion | flops 6586302464 | bytes 20279808 | tf_op jit(solution)/shard_map/b1_gw1/bsc,bsd->cd/dot_general | solution.py:421
  278.1 4.9 reshape.444
  286.3 8.8 %convert_reduce_fusion.8 = (f32[512]{0:T(512)S(1)}, f32[196]{0:T(256)S(1)}, f32[512]{0:T(512)S(1)}, f32[512]{0:T(512)S(1)}, bf16[16,196,512]{2,1,0:T(8,128)(2,1)S(1)}) fusion(f32[16,196]{1,0:T(8,128)S(1)} %add_multiply_fusion.7, f32[16,196]{1,0:T(8,128)S(1)} %multiply_multiply_fusion.7, f32[16,196]{1,0:T(8,128)S(1)} %broadcast_multiply_fusion, ...), kind=kLoop, calls=%fused_computation.62 | loop fusion | flops 41744700 | bytes 12989200 | tf_op jit(solution)/shard_map/reduce_sum | solution.py:445
  295.2 11.2 %fusion.124 = f32[256,196]{1,0:T(8,128)} fusion(bf16[16,196,512]{2,1,0:T(8,128)(2,1)S(1)} %get-tuple-element.76, f32[16,512,256]{2,1,0:T(8,128)} %copy-done.92, f32[256]{0:T(256)S(1)} %copy-done.89, bf16[16,196,512]{2,1,0:T(8,128)(2,1)S(1)} %get-tuple-element.111, f32[16,196]{1,0:T(8,128)S(1)} %add_multiply_fusion.7, ...), kind=kOutput, calls=%fused_computation.166 | convolution fusion | flops 860225536 | bytes 15097856 | tf_op jit(solution)/shard_map/b1_gt2/bcj,bsc->js/dot_general | solution.py:421
  306.4 10.1 %fusion.182 = (f32[256]{0:T(256)S(1)}, bf16[16,512,256]{2,1,0:T(8,128)(2,1)}) fusion(f32[16,512,256]{2,1,0:T(8,128)S(1)} %bitcast.219, f32[256]{0:T(256)S(1)} %copy-done.89, bf16[256,196]{1,0:T(8,128)(2,1)S(1)} %copy-done.42, bf16[16,196,512]{2,1,0:T(8,128)(2,1)S(1)} %get-tuple-element.76, f32[16,196]{1,0:T(8,128)S(1)} %add_multiply_fusion.7, ...), kind=kOutput, calls=%fused_computation.300 | convolution fusion | flops 883293952 | bytes 19192832 | tf_op jit(solution)/shard_map/b1_dtok/bsc,js->bcj/dot_general | solution.py:461
  318.4 5.6 fusion.127
  324.1 4.8 fusion.61
  336.8 10.2 %convert_add_fusion.6 = f32[16,196,512]{2,1,0:T(8,128)} fusion(bf16[16,196,512]{2,1,0:T(8,128)(2,1)} %copy-done.9, bf16[16,196,512]{2,1,0:T(8,128)(2,1)} %copy-done.4, bf16[196,16,512]{2,0,1:T(8,128)(2,1)} %get-tuple-element.115, f32[16,196]{1,0:T(8,128)S(1)} %add_multiply_fusion.5, f32[16,196]{1,0:T(8,128)S(1)} %multiply_multiply_fusion.5, ...), kind=kLoop, calls=%fused_computation.132 | loop fusion | flops 35323904 | bytes 19404800 | tf_op jit(solution)/shard_map/add | solution.py:468
  349.1 19.2 %convolution_bitcast_fusion.1 = f32[2048,512]{1,0:T(8,128)} fusion(f32[16,196,512]{2,1,0:T(8,128)} %convert_add_fusion.6, f32[16,196,2048]{2,1,0:T(8,128)} %fusion.108, f32[2048]{0:T(1024)S(1)} %copy-done.65), kind=kOutput, calls=%fused_computation.146 | convolution fusion | flops 6636077056 | bytes 36315136 | tf_op jit(solution)/shard_map/b0_gw2/bsd,bsc->dc/dot_general | solution.py:421
  368.3 22.8 %fusion.181 = (f32[2048]{0:T(1024)S(1)}, bf16[16,196,2048]{2,1,0:T(8,128)(2,1)}) fusion(f32[16,196,2048]{2,1,0:T(8,128)} %fusion.108, f32[2048]{0:T(1024)S(1)} %copy-done.65, bf16[2048,512,1]{1,0,2:T(8,128)(2,1)S(1)} %copy-done.18, f32[16,196,512]{2,1,0:T(8,128)S(1)} %bitcast.182), kind=kOutput, calls=%fused_computation.299 | convolution fusion | flops 6706722816 | bytes 47071232 | tf_op jit(solution)/shard_map/b0_dact/bsc,dc->bsd/dot_general | solution.py:448
  391.1 5.0 reshape.439
  396.2 15.5 %fusion.76 = (f32[512]{0:T(512)S(1)}, f32[16,196]{1,0:T(8,128)S(1)}, f32[16,196]{1,0:T(8,128)S(1)}, f32[512]{0:T(512)S(1)}, bf16[16,196,512]{2,1,0:T(8,128)(2,1)}) fusion(bf16[16,196,512]{2,1,0:T(8,128)(2,1)S(1)} %copy-done.3, f32[16,196]{1,0:T(8,128)S(1)} %copy-done.52, f32[16,196]{1,0:T(8,128)S(1)} %copy-done.30, f32[512]{0:T(512)S(1)} %copy-done.61, ...), kind=kOutput, calls=%fused_computation.126 | convolution fusion | flops 6597534720 | bytes 21421056 | tf_op jit(solution)/shard_map/b0_dnorm2/bsd,cd->bsc/dot_general | solution.py:421
  411.7 10.0 %fusion.92 = f32[512,2048]{1,0:T(8,128)} fusion(bf16[16,196,2048]{2,1,0:T(8,128)(2,1)S(1)} %copy-done.95, bf16[16,196,512]{2,1,0:T(8,128)(2,1)S(1)} %copy-done.3, f32[512]{0:T(512)S(1)} %copy-done.76, f32[512]{0:T(512)S(1)} %copy-done.61, f32[16,196]{1,0:T(8,128)S(1)} %copy-done.52, f32[16,196]{1,0:T(8,128)S(1)} %copy-done.30), kind=kOutput, calls=%fused_computation.144 | convolution fusion | flops 6586302464 | bytes 20279808 | tf_op jit(solution)/shard_map/b0_gw1/bsc,bsd->cd/dot_general | solution.py:421
  421.7 4.9 reshape.438
  428.5 7.2 %fusion.166 = (f32[512]{0:T(512)S(1)}, f32[196]{0:T(256)S(1)}, bf16[16,196,512]{2,1,0:T(8,128)(2,1)S(1)}) fusion(f32[16,196,512]{2,1,0:T(8,128)} %convert_add_fusion.6, f32[16,196]{1,0:T(8,128)S(1)} %add_multiply_fusion.4, f32[16,196]{1,0:T(8,128)S(1)} %multiply_multiply_fusion.4, f32[16,196]{1,0:T(8,128)S(1)} %copy-done.30, ...), kind=kLoop, calls=%fused_computation.290 | loop fusion | flops 20872508 | bytes 16111376 | tf_op jit(solution)/shard_map/reduce_sum | solution.py:445
  435.8 9.5 %convolution_bitcast_fusion.2 = f32[256,196]{1,0:T(8,128)} fusion(f32[16,196,512]{2,1,0:T(8,128)} %convert_add_fusion.6, bf16[16,196,512]{2,1,0:T(8,128)(2,1)S(1)} %get-tuple-element.77, f32[16,512,256]{2,1,0:T(8,128)} %copy-done.93, f32[256]{0:T(256)S(1)} %copy-done.87), kind=kOutput, calls=%fused_computation.167 | convolution fusion | flops 845774848 | bytes 18224128 | tf_op jit(solution)/shard_map/b0_gt2/bcj,bsc->js/dot_general | solution.py:421
  445.4 7.6 %fusion.180 = (f32[256]{0:T(256)S(1)}, bf16[16,512,256]{2,1,0:T(8,128)(2,1)}) fusion(f32[16,512,256]{2,1,0:T(8,128)S(1)} %bitcast.221, f32[256]{0:T(256)S(1)} %copy-done.87, bf16[256,196]{1,0:T(8,128)(2,1)S(1)} %copy-done.40, f32[16,196,512]{2,1,0:T(8,128)S(1)} %bitcast.184, bf16[16,196,512]{2,1,0:T(8,128)(2,1)S(1)} %get-tuple-element.77), kind=kOutput, calls=%fused_computation.298 | convolution fusion | flops 868843264 | bytes 22319104 | tf_op jit(solution)/shard_map/b0_dtok/bsc,js->bcj/dot_general | solution.py:461
  454.2 7.0 %fusion.132 = f32[196,256]{1,0:T(8,128)} fusion(bf16[16,512,256]{2,1,0:T(8,128)(2,1)} %get-tuple-element.120, f32[512]{0:T(512)S(1)} %copy-done.73, f32[512]{0:T(512)S(1)} %copy-done.74, f32[16,196]{1,0:T(8,128)S(1)} %copy-done.59, f32[16,196]{1,0:T(8,128)S(1)} %copy-done.50, bf16[16,196,512]{2,0,1:T(8,128)(2,1)S(1)} %copy-done.11), kind=kOutput, calls=%fused_computation.169 | convolution fusion | flops 831717376 | bytes 7635456 | tf_op jit(solution)/shard_map/b0_gt1/bsc,bcj->sj/dot_general | solution.py:421
  461.2 6.1 fusion.54
  484.7 132.4 %scatter_grads.1 = (f32[68,8,128]{2,1,0:T(8,128)}, f32[85,8,128]{2,1,0:T(8,128)}) custom-call(f32[8,269,8,128]{3,2,1,0:T(8,128)} %bitcast.187, f32[8,269,8,128]{3,2,1,0:T(8,128)} %bitcast.188, f32[32,17,8,128]{3,2,1,0:T(8,128)} %select_maximum_fusion.extra_ref), custom_call_target="tpu_custom_call" | custom-call | tf_op jit(solution)/shard_map/scatter_grads/pallas_call | solution.py:331
  628.3 9.3 %sum_over_devices.1 = f32[8,128]{1,0:T(8,128)} custom-call(f32[8,128]{1,0:T(8,128)} %scatter.9.x_ref), custom_call_target="tpu_custom_call" | custom-call | tf_op jit(solution)/shard_map/sum_over_devices/pallas_call | solution.py:379
  (345 shorter events, 130.9 us)
Async XLA Ops:
  98.0 13.8 %copy-start.10 = (bf16[16,196,512]{2,0,1:T(8,128)(2,1)S(1)}, bf16[16,196,512]{2,0,1:T(8,128)(2,1)}, u32[]{:S(2)}) copy-start(bf16[16,196,512]{2,0,1:T(8,128)(2,1)} %param.15) | copy-start | bytes 9633796
  102.3 15.3 %copy-start.43 = (bf16[196,256,1]{1,0,2:T(8,128)(2,1)}, bf16[196,256,1]{1,0,2:T(8,128)(2,1)S(1)}, u32[]{:S(2)}) copy-start(bf16[196,256,1]{1,0,2:T(8,128)(2,1)S(1)} %reshape.459) | copy-start | bytes 301060
  102.7 14.9 %copy-start.39 = (bf16[256,196]{1,0:T(8,128)(2,1)}, bf16[256,196]{1,0:T(8,128)(2,1)S(1)}, u32[]{:S(2)}) copy-start(bf16[256,196]{1,0:T(8,128)(2,1)S(1)} %reshape.422) | copy-start | bytes 301060
  123.9 15.4 %copy-start.2 = (bf16[16,196,512]{2,1,0:T(8,128)(2,1)}, bf16[16,196,512]{2,1,0:T(8,128)(2,1)S(1)}, u32[]{:S(2)}) copy-start(bf16[16,196,512]{2,1,0:T(8,128)(2,1)S(1)} %get-tuple-element.103) | copy-start | bytes 9633796
  139.3 19.4 %copy-start.45 = (bf16[196,256,1]{1,0,2:T(8,128)(2,1)S(1)}, bf16[196,256,1]{1,0,2:T(8,128)(2,1)}, u32[]{:S(2)}) copy-start(bf16[196,256,1]{1,0,2:T(8,128)(2,1)} %reshape.463) | copy-start | bytes 301060
  139.3 19.4 %copy-start.67 = (f32[512]{0:T(512)S(1)}, f32[512]{0:T(512)}, u32[]{:S(2)}) copy-start(f32[512]{0:T(512)} %get-tuple-element.92) | copy-start | bytes 6148
  139.3 19.4 %copy-start.77 = (f32[512]{0:T(512)S(1)}, f32[512]{0:T(512)}, u32[]{:S(2)}) copy-start(f32[512]{0:T(512)} %get-tuple-element.91) | copy-start | bytes 6148
  165.6 20.9 %copy-start = (bf16[16,196,512]{2,1,0:T(8,128)(2,1)}, bf16[16,196,512]{2,1,0:T(8,128)(2,1)S(1)}, u32[]{:S(2)}) copy-start(bf16[16,196,512]{2,1,0:T(8,128)(2,1)S(1)} %get-tuple-element.107) | copy-start | bytes 9633796
  167.2 19.3 %copy-start.80 = (f32[512]{0:T(512)S(1)}, f32[512]{0:T(512)}, u32[]{:S(2)}) copy-start(f32[512]{0:T(512)} %get-tuple-element.89) | copy-start | bytes 6148
  206.7 25.9 %slice-start.8 = ((s8[13107200]{0:T(1024)(128)(4,1)}), s8[524288]{0:T(1024)(128)(4,1)S(1)}, s32[]{:S(2)}) async-start(s8[13107200]{0:T(1024)(128)(4,1)} %bitcast.222), calls=%async_computation.8 | async-start | bytes 1048576
  208.4 24.2 %slice-start.9 = ((s8[13107200]{0:T(1024)(128)(4,1)}), s8[4194304]{0:T(1024)(128)(4,1)S(1)}, s32[]{:S(2)}) async-start(s8[13107200]{0:T(1024)(128)(4,1)} %bitcast.222), calls=%async_computation.9 | async-start | bytes 8388608
  208.4 24.2 %slice-start.10 = ((s8[13107200]{0:T(1024)(128)(4,1)}), s8[4194304]{0:T(1024)(128)(4,1)S(1)}, s32[]{:S(2)}) async-start(s8[13107200]{0:T(1024)(128)(4,1)} %bitcast.222), calls=%async_computation.10 | async-start | bytes 8388608
  208.4 24.2 %slice-start.11 = ((s8[13107200]{0:T(1024)(128)(4,1)}), s8[4194304]{0:T(1024)(128)(4,1)S(1)}, s32[]{:S(2)}) async-start(s8[13107200]{0:T(1024)(128)(4,1)} %bitcast.222), calls=%async_computation.11 | async-start | bytes 8388608
  247.2 16.4 %copy-start.1 = (bf16[16,196,512]{2,1,0:T(8,128)(2,1)S(1)}, bf16[16,196,512]{2,1,0:T(8,128)(2,1)}, u32[]{:S(2)}) copy-start(bf16[16,196,512]{2,1,0:T(8,128)(2,1)} %copy-done) | copy-start | bytes 9633796
  286.3 20.1 %slice-start.4 = ((s8[8388608]{0:T(1024)(128)(4,1)}), s8[4194304]{0:T(1024)(128)(4,1)S(1)}, s32[]{:S(2)}) async-start(s8[8388608]{0:T(1024)(128)(4,1)} %bitcast.218), calls=%async_computation.4 | async-start | bytes 8388608
  347.5 20.8 %slice-start = ((s8[6553600]{0:T(1024)(128)(4,1)}), s8[4194304]{0:T(1024)(128)(4,1)S(1)}, s32[]{:S(2)}) async-start(s8[6553600]{0:T(1024)(128)(4,1)} %bitcast.181), calls=%async_computation | async-start | bytes 8388608
  349.1 19.2 %slice-start.1 = ((s8[6553600]{0:T(1024)(128)(4,1)}), s8[2359296]{0:T(1024)(128)(4,1)S(1)}, s32[]{:S(2)}) async-start(s8[6553600]{0:T(1024)(128)(4,1)} %bitcast.181), calls=%async_computation.1 | async-start | bytes 4718592
  349.1 19.2 %copy-start.18 = (bf16[2048,512,1]{1,0,2:T(8,128)(2,1)S(1)}, bf16[2048,512,1]{1,0,2:T(8,128)(2,1)}, u32[]{:S(2)}) copy-start(bf16[2048,512,1]{1,0,2:T(8,128)(2,1)} %reshape.462) | copy-start | bytes 6291460
  396.2 15.5 %copy-start.76 = (f32[512]{0:T(512)S(1)}, f32[512]{0:T(512)}, u32[]{:S(2)}) copy-start(f32[512]{0:T(512)} %get-tuple-element.95) | copy-start | bytes 6148
  396.2 15.5 %copy-start.95 = (bf16[16,196,2048]{2,1,0:T(8,128)(2,1)S(1)}, bf16[16,196,2048]{2,1,0:T(8,128)(2,1)}, u32[]{:S(2)}) copy-start(bf16[16,196,2048]{2,1,0:T(8,128)(2,1)} %get-tuple-element.122) | copy-start | bytes 38535172
  428.5 16.8 %slice-start.2 = ((s8[6553600]{0:T(1024)(128)(4,1)}), s8[4194304]{0:T(1024)(128)(4,1)S(1)}, s32[]{:S(2)}) async-start(s8[6553600]{0:T(1024)(128)(4,1)} %bitcast.183), calls=%async_computation.2 | async-start | bytes 8388608
  428.5 16.8 %slice-start.6 = ((s8[8388608]{0:T(1024)(128)(4,1)}), s8[4194304]{0:T(1024)(128)(4,1)S(1)}, s32[]{:S(2)}) async-start(s8[8388608]{0:T(1024)(128)(4,1)} %bitcast.220), calls=%async_computation.6 | async-start | bytes 8388608
  484.7 155.6 %copy-start.83 = (f32[128]{0:T(128)S(1)}, f32[128]{0:T(128)}, u32[]{:S(2)}) copy-start(f32[128]{0:T(128)} %param.19) | copy-start | bytes 1540
  484.7 155.6 %copy-start.84 = (f32[128]{0:T(128)S(1)}, f32[128]{0:T(128)}, u32[]{:S(2)}) copy-start(f32[128]{0:T(128)} %param.22) | copy-start | bytes 1540
  484.7 155.6 %copy-start.85 = (f32[128]{0:T(128)S(1)}, f32[128]{0:T(128)}, u32[]{:S(2)}) copy-start(f32[128]{0:T(128)} %param.25) | copy-start | bytes 1540
  484.7 156.9 %copy-start.32 = (f32[16,1000]{1,0:T(8,128)S(1)}, f32[16,1000]{1,0:T(8,128)}, u32[]{:S(2)}) copy-start(f32[16,1000]{1,0:T(8,128)} %param.18) | copy-start | bytes 192004
  484.7 156.9 %copy-start.53 = (f32[16,1000]{1,0:T(8,128)S(1)}, f32[16,1000]{1,0:T(8,128)}, u32[]{:S(2)}) copy-start(f32[16,1000]{1,0:T(8,128)} %param.21) | copy-start | bytes 192004
  484.7 156.9 %copy-start.54 = (f32[16,1000]{1,0:T(8,128)S(1)}, f32[16,1000]{1,0:T(8,128)}, u32[]{:S(2)}) copy-start(f32[16,1000]{1,0:T(8,128)} %param.24) | copy-start | bytes 192004
  484.7 157.6 %copy-start.16 = (f32[2,68864]{1,0:T(2,128)S(1)}, f32[2,68864]{1,0:T(2,128)}, u32[]{:S(2)}) copy-start(f32[2,68864]{1,0:T(2,128)} %param.17) | copy-start | bytes 1652740
  484.7 157.5 %copy-start.22 = (f32[68864]{0:T(1024)S(1)}, f32[68864]{0:T(1024)}, u32[]{:S(2)}) copy-start(f32[68864]{0:T(1024)} %fusion.141) | copy-start | bytes 826372
  484.7 157.5 %copy-start.25 = (f32[2,68864]{1,0:T(2,128)S(1)}, f32[2,68864]{1,0:T(2,128)}, u32[]{:S(2)}) copy-start(f32[2,68864]{1,0:T(2,128)} %param.20) | copy-start | bytes 1652740
  484.7 157.5 %copy-start.26 = (f32[2,68864]{1,0:T(2,128)S(1)}, f32[2,68864]{1,0:T(2,128)}, u32[]{:S(2)}) copy-start(f32[2,68864]{1,0:T(2,128)} %param.23) | copy-start | bytes 1652740
  (77 other events, 519.3 us)
where the time goes:
time: 659 us; the launch traced here: 647 us
  matrix products  274 us (42%)
  Pallas kernels  197 us (30%)
  local copies, waits for them, and re-layouts  88.5 us (13%)
  other arithmetic  80.6 us (12%)
  between operations  7.23 us (1%)
    dot_general x16, matrix products, scoped(): return jnp.einsum(spec, lhs, rhs, **kwargs)  170 us
    pallas_call x1, Pallas kernels, scatter_grads(): pl.pallas_call(scatter_kernel, out_shape=tuple((jax.ShapeDtypeStruct((siz...  132 us
    pallas_call x1, Pallas kernels, gather_shares(): pl.pallas_call(gather_kernel, out_shape=(jax.ShapeDtypeStruct(flat, dtype...  55.1 us
    dot_general x2, matrix products, layer_backward(): jnp.einsum('bsc,dc->bsd', d_out_bf, w_ch2, preferred_element_type=jnp.flo...  46.9 us
    dot_general x2, matrix products, layer_forward(): jnp.einsum('bsd,dc->bsc', act_ch, w_ch2, preferred_element_type=jnp.float32)  28 us
    reshape x8, local copies, waits for them, and re-layouts, pack_tiles(): pieces = [grad.reshape(-1, ROWS, LANES) for grad in grads[:4]]  25.2 us
    reduce_sum x9, other arithmetic, layer_norm(): var_val = jnp.mean(jnp.square(x_f - mean_val), axis=-1, keepdims=True)  19.9 us
    unnamed x234, local copies, waits for them, and re-layouts  18.1 us

commit v1 on v0

--- a/solution.py
+++ b/solution.py
@@ -1,3 +1,4 @@
+import functools
 import math
 import jax
 import jax.numpy as jnp
@@ -58,15 +59,6 @@
         pieces.append(flat[start:start + shape_one[0]])
         start = start + shape_one[0]
     return pieces
-
-
-def pack_tiles(grads, flat_len):
-    pieces = [grad.reshape(-1, ROWS, LANES) for grad in grads[:4]]
-    used = sum(piece.shape[0] for piece in pieces) * TILE
-    vectors = jnp.concatenate(grads[4:])
-    vectors = jnp.pad(vectors, (0, flat_len - used - vectors.shape[0]))
-    pieces.append(vectors.reshape(-1, ROWS, LANES))
-    return jnp.concatenate(pieces, axis=0)
 
 
 def head_to_tiles(head):
@@ -299,11 +291,13 @@
             for side in range(2):
                 post(own[side].at[dist * 4], far_in[side].at[dist - 1], send_sems.at[3 + side, 12 + dist], far_sems.at[side, dist - 1], dist * MASK_Z)
 
-    for dist in dists:
-        fold_core(dist)
+    fold_core(3)
+    fold_core(2)
     fold_first(3)
+    fold_core(1)
     fold_first(2)
     fold_second(3)
+    fold_core(0)
     fold_first(1)
     fold_second(2)
     fold_first(0)
@@ -344,6 +338,86 @@
         compiler_params=pltpu.CompilerParams(collective_id=2, has_side_effects=True),
         name='scatter_grads',
     )(grad0, grad1, extra)
+
+
+NT_DIMS = (((1,), (1,)), ((), ()))
+NN_DIMS = (((1,), (0,)), ((), ()))
+HID_CHUNK = 512
+
+
+def mlp_grad_kernel(d_out_ref, act_ref, slope_ref, normed_ref, w1_ref, w2_ref, d_normed_ref, bias_ref, flat_ref, acc1, acc2, staged, sems, *, row1, row2):
+    step = pl.program_id(0)
+    chans, hid = acc1.shape
+
+    @pl.when(step == 0)
+    def _():
+        acc1[...] = jnp.zeros_like(acc1)
+        acc2[...] = jnp.zeros_like(acc2)
+        bias_ref[...] = jnp.zeros_like(bias_ref)
+
+    d_out = d_out_ref[...]
+    d_out_t = d_out.T
+    normed_t = normed_ref[...].T
+    d_normed = None
+    for start in range(0, hid, HID_CHUNK):
+        cols = pl.ds(start, HID_CHUNK)
+        d_act = lax.dot_general(d_out, w2_ref[cols, :], NT_DIMS, preferred_element_type=jnp.float32)
+        acc2[:, cols] += lax.dot_general(d_out_t, act_ref[:, cols], NN_DIMS, preferred_element_type=jnp.float32)
+        d_hid = d_act.astype(jnp.bfloat16).astype(jnp.float32) * slope_ref[:, cols]
+        bias_ref[:, cols] += jnp.sum(d_hid.reshape(-1, ROWS, HID_CHUNK), axis=0)
+        d_hid_bf = d_hid.astype(jnp.bfloat16)
+        acc1[:, cols] += lax.dot_general(normed_t, d_hid_bf, NN_DIMS, preferred_element_type=jnp.float32)
+        part = lax.dot_general(d_hid_bf, w1_ref[:, cols], NT_DIMS, preferred_element_type=jnp.float32)
+        d_normed = part if d_normed is None else d_normed + part
+    d_normed_ref[...] = d_normed.astype(d_normed_ref.dtype)
+
+    @pl.when(step == pl.num_programs(0) - 1)
+    def _():
+        wide = hid // LANES
+        for col in range(wide):
+            staged[0, pl.ds(col, chans, stride=wide), :] = acc1[:, col * LANES:(col + 1) * LANES]
+        first = pltpu.make_async_copy(staged.at[0], flat_ref.at[pl.ds(row1, chans * wide)], sems.at[0])
+        first.start()
+        narrow = chans // LANES
+        for col in range(narrow):
+            staged[1, pl.ds(col, hid, stride=narrow), :] = acc2[col * LANES:(col + 1) * LANES, :].T
+        second = pltpu.make_async_copy(staged.at[1], flat_ref.at[pl.ds(row2, chans * wide)], sems.at[1])
+        second.start()
+        first.wait()
+        second.wait()
+
+
+def mlp_grad(d_out, act, slope, normed, w1, w2, flat_rows, row1, row2, block):
+    tokens, chans = d_out.shape
+    hid = act.shape[1]
+
+    def by_block(width):
+        return pl.BlockSpec((block, width), lambda step: (step, 0))
+
+    def whole(shape):
+        return pl.BlockSpec(shape, lambda step: (0, 0), pipeline_mode=pl.Buffered(1))
+
+    mat_rows = chans * hid // LANES
+    return pl.pallas_call(
+        functools.partial(mlp_grad_kernel, row1=row1, row2=row2),
+        grid=(tokens // block,),
+        out_shape=(
+            jax.ShapeDtypeStruct((tokens, chans), jnp.bfloat16),
+            jax.ShapeDtypeStruct((ROWS, hid), jnp.float32),
+            jax.ShapeDtypeStruct((flat_rows, LANES), jnp.float32),
+        ),
+        in_specs=[by_block(chans), by_block(hid), by_block(hid), by_block(chans), whole(w1.shape), whole(w2.shape)],
+        out_specs=(by_block(chans), pl.BlockSpec((ROWS, hid), lambda step: (0, 0)), pl.BlockSpec(memory_space=pl.ANY)),
+        scratch_shapes=[
+            pltpu.VMEM((chans, hid), jnp.float32),
+            pltpu.VMEM((chans, hid), jnp.float32),
+            pltpu.VMEM((2, mat_rows, LANES), jnp.float32),
+            pltpu.SemaphoreType.DMA((2,)),
+        ],
+        compiler_params=pltpu.CompilerParams(dimension_semantics=('arbitrary',), vmem_limit_bytes=60 * 1024 * 1024),
+        cost_estimate=pl.CostEstimate(flops=8 * tokens * chans * hid, bytes_accessed=6 * tokens * hid + 6 * tokens * chans + 12 * chans * hid, transcendentals=0),
+        name='mlp_grad',
+    )(d_out, act, slope, normed, w1, w2)
 
 
 def sum_kernel(x_ref, out_ref, held, local_sem, send_sems, recv_sems):
@@ -438,19 +512,20 @@
     return layer_out, (x_in, normed, slope_tok, act_tok, after_tok, normed2, slope_ch, act_ch)
 
 
-def layer_backward(d_out, weights, cache, tag):
+def layer_backward(d_out, weights, cache, tag, flat_len):
+    num_tokens, num_chans = d_out.shape[1:]
     w_tok1, w_tok2, w_ch1, w_ch2, ln1_g, ln1_b, b_tok1, b_tok2, ln2_g, ln2_b, b_ch1, b_ch2 = weights
     x_in, normed, slope_tok, act_tok, after_tok, normed2, slope_ch, act_ch = cache
     d_out_bf = d_out.astype(jnp.bfloat16)
     g_b_ch2 = jnp.sum(d_out, axis=(0, 1))
-    g_w_ch2 = scoped(tag + '_gw2', 'bsd,bsc->dc', act_ch, d_out_bf, preferred_element_type=jnp.float32)
-    with jax.named_scope(tag + '_dact'):
-        d_act_ch = jnp.einsum('bsc,dc->bsd', d_out_bf, w_ch2, preferred_element_type=jnp.float32)
-        d_hid_ch = d_act_ch.astype(jnp.bfloat16).astype(jnp.float32) * slope_ch
-        d_hid_ch_bf = d_hid_ch.astype(jnp.bfloat16)
-        g_b_ch1 = jnp.sum(d_hid_ch, axis=(0, 1))
-    g_w_ch1 = scoped(tag + '_gw1', 'bsc,bsd->cd', normed2, d_hid_ch_bf, preferred_element_type=jnp.float32)
-    d_normed2 = scoped(tag + '_dnorm2', 'bsd,cd->bsc', d_hid_ch_bf, w_ch1, preferred_element_type=jnp.float32)
+    tokens = d_out.shape[0] * num_tokens
+    mat_tiles = [math.prod(shape_one) // LANES for shape_one in piece_shapes(num_tokens, num_chans)[:4]]
+    row1 = mat_tiles[0] + mat_tiles[1]
+    d_normed2, bias_rows, flat_grad = mlp_grad(
+        d_out_bf.reshape(tokens, num_chans), act_ch.reshape(tokens, -1), slope_ch.reshape(tokens, -1), normed2.reshape(tokens, num_chans),
+        w_ch1, w_ch2, flat_len // LANES, row1, row1 + mat_tiles[2], tokens // 7)
+    g_b_ch1 = jnp.sum(bias_rows, axis=0)
+    d_normed2 = d_normed2.reshape(d_out.shape)
     with jax.named_scope(tag + '_ln2'):
         d_after_ln, g_ln2_g, g_ln2_b = norm_grad(after_tok, ln2_g, ln2_b, d_normed2)
     d_after = d_after_ln + d_out
@@ -466,7 +541,13 @@
     d_normed = scoped(tag + '_dnt', 'bcj,sj->bsc', d_hid_tok_bf, w_tok1, preferred_element_type=jnp.float32)
     d_in_ln, g_ln1_g, g_ln1_b = norm_grad(x_in, ln1_g, ln1_b, d_normed)
     d_in = d_in_ln + d_after
-    return d_in, [g_w_tok1, g_w_tok2, g_w_ch1, g_w_ch2, g_ln1_g, g_ln1_b, g_b_tok1, g_b_tok2, g_ln2_g, g_ln2_b, g_b_ch1, g_b_ch2]
+    vectors = jnp.concatenate([g_ln1_g, g_ln1_b, g_b_tok1, g_b_tok2, g_ln2_g, g_ln2_b, g_b_ch1, g_b_ch2])
+    last_row = row1 + mat_tiles[2] + mat_tiles[3]
+    vectors = jnp.pad(vectors, (0, flat_len - last_row * LANES - vectors.shape[0])).reshape(-1, LANES)
+    tok_rows = jnp.concatenate([g_w_tok1.reshape(-1, LANES), g_w_tok2.reshape(-1, LANES)], axis=0)
+    flat_grad = lax.dynamic_update_slice(flat_grad, tok_rows, (0, 0))
+    flat_grad = lax.dynamic_update_slice(flat_grad, vectors, (last_row, 0))
+    return d_in, flat_grad
 
 
 def head_step(hidden, labels, small_full, head_full, num_classes, global_b):
@@ -542,8 +623,8 @@
         small_blocks = jnp.pad(g_small, ((0, 0), (0, 0), (0, ROWS - 1), (0, 0)))
         packed = [None] * num_layers
         for layer_idx in reversed(range(num_layers)):
-            d_hidden, grads = layer_backward(d_hidden, weights[layer_idx], caches[layer_idx], f'b{layer_idx}')
-            packed[layer_idx] = pack_tiles(grads, flat_len).reshape(flat0.shape)
+            d_hidden, flat_grad = layer_backward(d_hidden, weights[layer_idx], caches[layer_idx], f'b{layer_idx}', flat_len)
+            packed[layer_idx] = flat_grad.reshape(flat0.shape)
         summed0, summed1 = scatter_grads(packed[0], packed[1], jnp.concatenate([head_blocks, small_blocks], axis=1), win_tiles)
         layer_g = jnp.stack([window_to_share(summed0, share_len), window_to_share(summed1[:win_tiles], share_len)])
         head_g = tiles_to_head(summed1[win_tiles:win_tiles + num_head], head_rows)[:, :num_classes]

time: 659 us -> 687 us (1.042)
  matrix products: 274 us -> 142 us
  local copies, waits for them, and re-layouts: 88.5 us -> 160 us
  Pallas kernels: 197 us -> 264 us
  other arithmetic: 80.6 us -> 108 us
    pallas_call x0 -> x2, Pallas kernels: none -> 84.2 us  [mlp_grad(): pl.pallas_call(functools.partial(mlp_grad_kernel, row1=row1, row2=row2),...]
    dot_general x16 -> x10, matrix products: 170 us -> 90 us  [scoped(): return jnp.einsum(spec, lhs, rhs, **kwargs)]
    reshape x8 -> x12, local copies, waits for them, and re-layouts: 25.2 us -> 85.4 us  [the longest x2 38.1 us: layer_backward(): slope_ch.reshape(tokens, -1)]
    dot_general x2 -> x0, matrix products: 46.9 us -> none  [layer_backward(): jnp.einsum('bsc,dc->bsd', d_out_bf, w_ch2, preferred_element_type=jnp.flo...]
    reduce_sum x2 -> x7, other arithmetic: 4.87 us -> 28 us  [layer_norm(): normed * ln_gain.astype(jnp.float32) + ln_shift.astype(jnp.float32)]
    convert_element_type x0 -> x4, other arithmetic: none -> 18.6 us  [the longest x1 9.58 us: layer_backward(): d_out_bf = d_out.astype(jnp.bfloat16)]
    pallas_call x1, Pallas kernels: 132 us -> 116 us  [scatter_grads(): pl.pallas_call(scatter_kernel, out_shape=tuple((jax.ShapeDtypeStruct((siz...]
    unnamed x234 -> x196, local copies, waits for them, and re-layouts: 18.1 us -> 3.25 us
where the time goes in v1:
time: 687 us; the launch traced here: 681 us
  Pallas kernels  264 us (38%)
  local copies, waits for them, and re-layouts  160 us (23%)
  matrix products  142 us (21%)
  other arithmetic  108 us (16%)
    pallas_call x1, Pallas kernels, scatter_grads(): pl.pallas_call(scatter_kernel, out_shape=tuple((jax.ShapeDtypeStruct((siz...  116 us
    dot_general x10, matrix products, scoped(): return jnp.einsum(spec, lhs, rhs, **kwargs)  90 us
    pallas_call x2, Pallas kernels, mlp_grad(): pl.pallas_call(functools.partial(mlp_grad_kernel, row1=row1, row2=row2),...  84.2 us
    pallas_call x1, Pallas kernels, gather_shares(): pl.pallas_call(gather_kernel, out_shape=(jax.ShapeDtypeStruct(flat, dtype...  55.1 us
    reshape x2, local copies, waits for them, and re-layouts, layer_backward(): slope_ch.reshape(tokens, -1)  38.1 us
    reshape x12, local copies, waits for them, and re-layouts, unpack_tiles(): pieces.append(tiles[start:start + count].reshape(shape_one))  31.9 us
    reduce_sum x7, other arithmetic, layer_norm(): normed * ln_gain.astype(jnp.float32) + ln_shift.astype(jnp.float32)  28 us
    reshape x2, local copies, waits for them, and re-layouts, layer_backward(): act_ch.reshape(tokens, -1)  24.7 us

profile of v1, /device:TPU:0, one launch (start us, length us, event | category | flops | bytes accessed | tf_op | source)
XLA Modules:
  0.0 681.1 jit_solution(15340829126409185283)
XLA Ops:
  2.5 5.3 convert_reduce_fusion.3
  16.9 55.1 %gather_shares.1 = (bf16[8,269,8,128]{3,2,1,0:T(8,128)(2,1)}, bf16[8,269,8,128]{3,2,1,0:T(8,128)(2,1)}, bf16[32,17,8,128]{3,2,1,0:T(8,128)(2,1)}) custom-call(bf16[66,8,128]{2,1,0:T(8,128)(2,1)} %slice_bitcast_fusion.2.inner0_ref, bf16[66,8,128]{2,1,0:T(8,128)(2,1)} %slice_bitcast_fusion.1.inner1_ref, bf16[21,8,128]{2,1,0:T(8,128)(2,1)} %copy-done.55), custom_call_target="tpu_custom_call" | custom-call | tf_op jit(solution)/shard_map/gather_shares/pallas_call | solution.py:196
  90.5 4.5 fusion.142
  125.9 6.1 fusion.89
  132.1 6.4 convert_reduce_fusion.2
  148.9 24.2 %multiply_add_fusion = (f32[16,196,2048]{2,1,0:T(8,128)}, bf16[16,196,2048]{2,1,0:T(8,128)(2,1)}) fusion(f32[2048]{0:T(1024)S(1)} %copy-done.66, bf16[16,196,512]{2,1,0:T(8,128)(2,1)} %fusion.49, bf16[512,2048,1]{1,0,2:T(8,128)(2,1)} %reshape.505), kind=kOutput, calls=%fused_computation | convolution fusion | flops 6685851648 | bytes 43851776 | tf_op jit(solution)/shard_map/f0_ch1/bsc,cd->bsd/dot_general | solution.py:495
  173.1 19.0 %reshape.480.slope_ref = f32[3136,2048]{1,0:T(8,128)} reshape(f32[16,196,2048]{2,1,0:T(8,128)} %get-tuple-element.92) | data formatting | bytes 51380224 | tf_op jit(solution)/shard_map/reshape | solution.py:525
  192.2 12.8 %convert_reduce_fusion.1 = (f32[16,196]{1,0:T(8,128)S(1)}, bf16[16,196,512]{2,1,0:T(8,128)(2,1)}) fusion(f32[512]{0:T(512)S(1)} %copy-done.75, bf16[16,196,2048]{2,1,0:T(8,128)(2,1)} %get-tuple-element.93, bf16[2048,512,1]{1,0,2:T(8,128)(2,1)} %reshape.506, bf16[16,196,512]{2,1,0:T(8,128)(2,1)S(1)} %get-tuple-element.121), kind=kOutput, calls=%fused_computation.19 | convolution fusion | flops 6586299392 | bytes 21379328 | tf_op jit(solution)/shard_map/f0_ch2/bsd,dc->bsc/dot_general | solution.py:510
  205.0 12.5 %reshape.479.act_ref = bf16[3136,2048]{1,0:T(8,128)(2,1)} reshape(bf16[16,196,2048]{2,1,0:T(8,128)(2,1)} %get-tuple-element.93) | data formatting | bytes 25690112 | tf_op jit(solution)/shard_map/reshape | solution.py:525
  230.7 4.4 reshape.477.normed_ref
  235.2 24.4 %multiply_add_fusion.1 = (f32[16,196,2048]{2,1,0:T(8,128)}, bf16[16,196,2048]{2,1,0:T(8,128)(2,1)}) fusion(f32[2048]{0:T(1024)S(1)} %copy-done.65, bf16[16,196,512]{2,1,0:T(8,128)(2,1)} %fusion.42, bf16[512,2048,1]{1,0,2:T(8,128)(2,1)} %reshape.509), kind=kOutput, calls=%fused_computation.1 | convolution fusion | flops 6685851648 | bytes 43851776 | tf_op jit(solution)/shard_map/f1_ch1/bsc,cd->bsd/dot_general | solution.py:495
  259.6 19.0 %reshape.476.slope_ref = f32[3136,2048]{1,0:T(8,128)} reshape(f32[16,196,2048]{2,1,0:T(8,128)} %get-tuple-element.94) | data formatting | bytes 51380224 | tf_op jit(solution)/shard_map/reshape | solution.py:525
  278.6 11.8 %convert_reduce_fusion.7 = (f32[16,196]{1,0:T(8,128)S(1)}, bf16[16,196,512]{2,1,0:T(8,128)(2,1)S(1)}) fusion(f32[512]{0:T(512)S(1)} %copy-done.74, bf16[16,196,2048]{2,1,0:T(8,128)(2,1)} %get-tuple-element.95, bf16[2048,512,1]{1,0,2:T(8,128)(2,1)} %reshape.510, bf16[16,196,512]{2,1,0:T(8,128)(2,1)} %copy-done), kind=kOutput, calls=%fused_computation.57 | convolution fusion | flops 6586299392 | bytes 21379328 | tf_op jit(solution)/shard_map/f1_ch2/bsd,dc->bsc/dot_general | solution.py:510
  290.4 12.3 %reshape.475.act_ref = bf16[3136,2048]{1,0:T(8,128)(2,1)} reshape(bf16[16,196,2048]{2,1,0:T(8,128)(2,1)} %get-tuple-element.95) | data formatting | bytes 25690112 | tf_op jit(solution)/shard_map/reshape | solution.py:525
  319.7 4.4 reshape.474.d_out_ref
  324.1 42.0 %mlp_grad.2 = (bf16[3136,512]{1,0:T(8,128)(2,1)}, f32[8,2048]{1,0:T(8,128)}, f32[17216,128]{1,0:T(8,128)}) custom-call(bf16[3136,512]{1,0:T(8,128)(2,1)} %reshape.474.d_out_ref, bf16[3136,2048]{1,0:T(8,128)(2,1)} %reshape.475.act_ref, f32[3136,2048]{1,0:T(8,128)} %reshape.476.slope_ref, bf16[3136,512]{1,0:T(8,128)(2,1)} %reshape.477.normed_ref, ...), custom_call_target="tpu_custom_call" | custom-call | flops 26306674688 | bytes 60751872 | tf_op jit(solution)/shard_map/mlp_grad/pallas_call | solution.py:401
  372.1 5.2 reshape.501
  377.3 6.4 fusion.43
  385.4 6.7 convert_reduce_fusion.6
  396.5 8.0 %fusion.148 = (f32[256]{0:T(256)}, bf16[16,512,256]{2,1,0:T(8,128)(2,1)}) fusion(f32[16,512,256]{2,1,0:T(8,128)S(1)} %bitcast.199, f32[256]{0:T(256)S(1)} %copy-done.83, bf16[256,196]{1,0:T(8,128)(2,1)S(1)} %copy-done.39, bf16[16,196,512]{2,1,0:T(8,128)(2,1)S(1)} %copy-done.11, bf16[16,196,512]{2,1,0:T(8,128)(2,1)S(1)} %get-tuple-element.88), kind=kOutput, calls=%fused_computation.270 | convolution fusion | flops 870448896 | bytes 19107840 | tf_op jit(solution)/shard_map/b1_dtok/bsc,js->bcj/dot_general | solution.py:536
  405.7 5.7 fusion.97
  411.5 5.3 fusion.61
  428.0 9.6 %fusion.139 = (bf16[16,196,512]{2,1,0:T(8,128)(2,1)}, f32[16,196,512]{2,1,0:T(8,128)}) fusion(bf16[16,196,512]{2,1,0:T(8,128)(2,1)} %copy-done.10, f32[16,196]{1,0:T(8,128)S(1)} %add_multiply_fusion.3, f32[16,196]{1,0:T(8,128)S(1)} %multiply_multiply_fusion.5, f32[16,196]{1,0:T(8,128)S(1)} %copy-done.30, bf16[16,196,512]{2,1,0:T(8,128)(2,1)} %get-tuple-element.123, ...), kind=kLoop, calls=%fused_computation.261 | loop fusion | flops 36929536 | bytes 22616064 | tf_op jit(solution)/shard_map/convert_element_type | solution.py:519
  437.6 4.4 reshape.478.d_out_ref
  442.0 42.1 %mlp_grad.3 = (bf16[3136,512]{1,0:T(8,128)(2,1)}, f32[8,2048]{1,0:T(8,128)}, f32[17216,128]{1,0:T(8,128)}) custom-call(bf16[3136,512]{1,0:T(8,128)(2,1)} %reshape.478.d_out_ref, bf16[3136,2048]{1,0:T(8,128)(2,1)} %reshape.479.act_ref, f32[3136,2048]{1,0:T(8,128)} %reshape.480.slope_ref, bf16[3136,512]{1,0:T(8,128)(2,1)} %reshape.481.normed_ref, ...), custom_call_target="tpu_custom_call" | custom-call | flops 26306674688 | bytes 60751872 | tf_op jit(solution)/shard_map/mlp_grad/pallas_call | solution.py:401
  489.1 5.2 reshape.502
  494.4 4.9 fusion.50
  508.8 7.5 %fusion.147 = (f32[256]{0:T(256)S(1)}, bf16[16,512,256]{2,1,0:T(8,128)(2,1)}) fusion(f32[16,512,256]{2,1,0:T(8,128)S(1)} %bitcast.201, f32[256]{0:T(256)S(1)} %copy-done.81, bf16[256,196]{1,0:T(8,128)(2,1)S(1)} %copy-done.37, f32[16,196,512]{2,1,0:T(8,128)S(1)} %copy-done.9, bf16[16,196,512]{2,1,0:T(8,128)(2,1)S(1)} %get-tuple-element.89), kind=kOutput, calls=%fused_computation.269 | convolution fusion | flops 868843264 | bytes 22319104 | tf_op jit(solution)/shard_map/b0_dtok/bsc,js->bcj/dot_general | solution.py:536
  517.5 7.0 %fusion.102 = f32[196,256]{1,0:T(8,128)} fusion(bf16[16,512,256]{2,1,0:T(8,128)(2,1)} %get-tuple-element.134, f32[512]{0:T(512)S(1)} %copy-done.69, f32[512]{0:T(512)S(1)} %copy-done.71, f32[16,196]{1,0:T(8,128)S(1)} %copy-done.60, f32[16,196]{1,0:T(8,128)S(1)} %copy-done.46, bf16[16,196,512]{2,0,1:T(8,128)(2,1)S(1)} %copy-done.13), kind=kOutput, calls=%fused_computation.145 | convolution fusion | flops 831717376 | bytes 7635456 | tf_op jit(solution)/shard_map/b0_gt1/bsc,bcj->sj/dot_general | solution.py:495
  524.6 6.1 fusion.58
  535.6 115.6 %scatter_grads.1 = (f32[68,8,128]{2,1,0:T(8,128)}, f32[85,8,128]{2,1,0:T(8,128)}) custom-call(f32[8,269,8,128]{3,2,1,0:T(8,128)} %bitcast.170, f32[8,269,8,128]{3,2,1,0:T(8,128)} %bitcast.171, f32[32,17,8,128]{3,2,1,0:T(8,128)} %select_maximum_fusion.extra_ref), custom_call_target="tpu_custom_call" | custom-call | tf_op jit(solution)/shard_map/scatter_grads/pallas_call | solution.py:325
  662.3 9.3 %sum_over_devices.1 = f32[8,128]{1,0:T(8,128)} custom-call(f32[8,128]{1,0:T(8,128)} %scatter.9.x_ref), custom_call_target="tpu_custom_call" | custom-call | tf_op jit(solution)/shard_map/sum_over_devices/pallas_call | solution.py:453
  (325 shorter events, 161.1 us)
Async XLA Ops:
  7.9 118.0 %copy-start.45 = (f32[16,196]{1,0:T(8,128)}, f32[16,196]{1,0:T(8,128)S(1)}, u32[]{:S(2)}) copy-start(f32[16,196]{1,0:T(8,128)S(1)} %broadcast_multiply_fusion.4) | copy-start | bytes 37636
  12.0 113.9 %copy-start.59 = (f32[16,196]{1,0:T(8,128)}, f32[16,196]{1,0:T(8,128)S(1)}, u32[]{:S(2)}) copy-start(f32[16,196]{1,0:T(8,128)S(1)} %add_rsqrt_fusion) | copy-start | bytes 37636
  80.3 139.3 %copy-start.61 = (f32[512]{0:T(512)}, f32[512]{0:T(512)S(1)}, u32[]{:S(2)}) copy-start(f32[512]{0:T(512)S(1)} %get-tuple-element.110) | copy-start | bytes 6148
  83.6 42.3 %copy-start.68 = (f32[512]{0:T(512)}, f32[512]{0:T(512)S(1)}, u32[]{:S(2)}) copy-start(f32[512]{0:T(512)S(1)} %get-tuple-element.114) | copy-start | bytes 6148
  83.6 42.3 %copy-start.70 = (f32[512]{0:T(512)}, f32[512]{0:T(512)S(1)}, u32[]{:S(2)}) copy-start(f32[512]{0:T(512)S(1)} %get-tuple-element.115) | copy-start | bytes 6148
  83.6 57.8 %copy-start.53 = (f32[512]{0:T(512)}, f32[512]{0:T(512)S(1)}, u32[]{:S(2)}) copy-start(f32[512]{0:T(512)S(1)} %get-tuple-element.111) | copy-start | bytes 6148
  89.5 132.8 %copy-start.38 = (bf16[256,196]{1,0:T(8,128)(2,1)}, bf16[256,196]{1,0:T(8,128)(2,1)S(1)}, u32[]{:S(2)}) copy-start(bf16[256,196]{1,0:T(8,128)(2,1)S(1)} %reshape.466) | copy-start | bytes 301060
  95.0 30.9 %copy-start.40 = (bf16[196,256,1]{1,0,2:T(8,128)(2,1)}, bf16[196,256,1]{1,0,2:T(8,128)(2,1)S(1)}, u32[]{:S(2)}) copy-start(bf16[196,256,1]{1,0,2:T(8,128)(2,1)S(1)} %reshape.503) | copy-start | bytes 301060
  95.4 36.6 %copy-start.36 = (bf16[256,196]{1,0:T(8,128)(2,1)}, bf16[256,196]{1,0:T(8,128)(2,1)S(1)}, u32[]{:S(2)}) copy-start(bf16[256,196]{1,0:T(8,128)(2,1)S(1)} %reshape.460) | copy-start | bytes 301060
  138.5 53.7 %copy-start.2 = (bf16[16,196,512]{2,1,0:T(8,128)(2,1)}, bf16[16,196,512]{2,1,0:T(8,128)(2,1)S(1)}, u32[]{:S(2)}) copy-start(bf16[16,196,512]{2,1,0:T(8,128)(2,1)S(1)} %get-tuple-element.121) | copy-start | bytes 9633796
  173.1 19.1 %copy-start.75 = (f32[512]{0:T(512)S(1)}, f32[512]{0:T(512)}, u32[]{:S(2)}) copy-start(f32[512]{0:T(512)} %get-tuple-element.112) | copy-start | bytes 6148
  205.0 12.5 %copy-start.6 = (bf16[16,196,512]{2,1,0:T(8,128)(2,1)S(1)}, bf16[16,196,512]{2,1,0:T(8,128)(2,1)}, u32[]{:S(2)}) copy-start(bf16[16,196,512]{2,1,0:T(8,128)(2,1)} %get-tuple-element.123) | copy-start | bytes 9633796
  205.0 14.6 %copy-start.42 = (bf16[196,256,1]{1,0,2:T(8,128)(2,1)S(1)}, bf16[196,256,1]{1,0,2:T(8,128)(2,1)}, u32[]{:S(2)}) copy-start(bf16[196,256,1]{1,0,2:T(8,128)(2,1)} %reshape.507) | copy-start | bytes 301060
  205.0 14.6 %copy-start.72 = (f32[512]{0:T(512)S(1)}, f32[512]{0:T(512)}, u32[]{:S(2)}) copy-start(f32[512]{0:T(512)} %get-tuple-element.109) | copy-start | bytes 6148
  259.6 19.0 %copy-start.74 = (f32[512]{0:T(512)S(1)}, f32[512]{0:T(512)}, u32[]{:S(2)}) copy-start(f32[512]{0:T(512)} %get-tuple-element.107) | copy-start | bytes 6148
  290.4 13.8 %copy-start.44 = (f32[4,1,1,128]{3,2,1,0:T(1,128)S(1)}, f32[4,1,1,128]{3,2,1,0:T(1,128)}, u32[]{:S(2)}) copy-start(f32[4,1,1,128]{3,2,1,0:T(1,128)} %get-tuple-element.104) | copy-start | bytes 6148
  290.4 13.8 %copy-start.64 = (f32[4,1,1,128]{3,2,1,0:T(1,128)S(1)}, f32[4,1,1,128]{3,2,1,0:T(1,128)}, u32[]{:S(2)}) copy-start(f32[4,1,1,128]{3,2,1,0:T(1,128)} %get-tuple-element.105) | copy-start | bytes 6148
  312.4 72.9 %copy-start.22 = (f32[16,196]{1,0:T(8,128)}, f32[16,196]{1,0:T(8,128)S(1)}, u32[]{:S(2)}) copy-start(f32[16,196]{1,0:T(8,128)S(1)} %multiply_multiply_fusion.7) | copy-start | bytes 37636
  314.4 71.0 %copy-start.26 = (f32[16,196]{1,0:T(8,128)}, f32[16,196]{1,0:T(8,128)S(1)}, u32[]{:S(2)}) copy-start(f32[16,196]{1,0:T(8,128)S(1)} %add_multiply_fusion.5) | copy-start | bytes 37636
  377.3 14.8 %slice-start = ((s8[8388608]{0:T(1024)(128)(4,1)}), s8[4194304]{0:T(1024)(128)(4,1)S(1)}, s32[]{:S(2)}) async-start(s8[8388608]{0:T(1024)(128)(4,1)} %bitcast.198), calls=%async_computation | async-start | bytes 8388608
  442.0 42.1 %copy-start.47 = (f32[3136]{0:T(1024)S(1)}, f32[3136]{0:T(1024)}, u32[]{:S(2)}) copy-start(f32[3136]{0:T(1024)} %rsqrt.67) | copy-start | bytes 37636
  442.0 42.1 %copy-start.54 = (f32[512]{0:T(512)S(1)}, f32[512]{0:T(512)}, u32[]{:S(2)}) copy-start(f32[512]{0:T(512)} %copy-done.53) | copy-start | bytes 6148
  535.5 138.7 %copy-start.77 = (f32[128]{0:T(128)S(1)}, f32[128]{0:T(128)}, u32[]{:S(2)}) copy-start(f32[128]{0:T(128)} %param.19) | copy-start | bytes 1540
  535.5 138.8 %copy-start.78 = (f32[128]{0:T(128)S(1)}, f32[128]{0:T(128)}, u32[]{:S(2)}) copy-start(f32[128]{0:T(128)} %param.22) | copy-start | bytes 1540
  535.6 138.8 %copy-start.79 = (f32[128]{0:T(128)S(1)}, f32[128]{0:T(128)}, u32[]{:S(2)}) copy-start(f32[128]{0:T(128)} %param.25) | copy-start | bytes 1540
  535.6 140.0 %copy-start.32 = (f32[16,1000]{1,0:T(8,128)S(1)}, f32[16,1000]{1,0:T(8,128)}, u32[]{:S(2)}) copy-start(f32[16,1000]{1,0:T(8,128)} %param.18) | copy-start | bytes 192004
  535.6 140.0 %copy-start.51 = (f32[16,1000]{1,0:T(8,128)S(1)}, f32[16,1000]{1,0:T(8,128)}, u32[]{:S(2)}) copy-start(f32[16,1000]{1,0:T(8,128)} %param.21) | copy-start | bytes 192004
  535.6 140.0 %copy-start.52 = (f32[16,1000]{1,0:T(8,128)S(1)}, f32[16,1000]{1,0:T(8,128)}, u32[]{:S(2)}) copy-start(f32[16,1000]{1,0:T(8,128)} %param.24) | copy-start | bytes 192004
  535.6 140.7 %copy-start.16 = (f32[2,68864]{1,0:T(2,128)S(1)}, f32[2,68864]{1,0:T(2,128)}, u32[]{:S(2)}) copy-start(f32[2,68864]{1,0:T(2,128)} %param.17) | copy-start | bytes 1652740
  535.6 140.7 %copy-start.17 = (f32[68864]{0:T(1024)S(1)}, f32[68864]{0:T(1024)}, u32[]{:S(2)}) copy-start(f32[68864]{0:T(1024)} %fusion.111) | copy-start | bytes 826372
  535.6 140.7 %copy-start.20 = (f32[2,68864]{1,0:T(2,128)S(1)}, f32[2,68864]{1,0:T(2,128)}, u32[]{:S(2)}) copy-start(f32[2,68864]{1,0:T(2,128)} %param.20) | copy-start | bytes 1652740
  535.6 140.7 %copy-start.21 = (f32[2,68864]{1,0:T(2,128)S(1)}, f32[2,68864]{1,0:T(2,128)}, u32[]{:S(2)}) copy-start(f32[2,68864]{1,0:T(2,128)} %param.23) | copy-start | bytes 1652740
  (62 other events, 407.1 us)

commit v2 on v1

--- a/solution.py
+++ b/solution.py
@@ -20,6 +20,7 @@
 LANES = 128
 TILE = ROWS * LANES
 HEAD_PAD = 1024
+IMAGE_ROWS = 8
 
 def row_offset(share_rows):
     return (lax.axis_index(AXIS) * share_rows) % ROWS
@@ -43,6 +44,12 @@
     tok_hid = num_chans // 2
     ch_hid = 4 * num_chans
     return [(num_tokens, tok_hid), (tok_hid, num_tokens), (num_chans, ch_hid), (ch_hid, num_chans), (num_chans,), (num_chans,), (tok_hid,), (num_tokens,), (num_chans,), (num_chans,), (ch_hid,), (num_chans,)]
+
+
+def pad_tokens(val, axis, num_tokens):
+    widths = [(0, 0)] * val.ndim
+    widths[axis] = (0, -num_tokens % IMAGE_ROWS)
+    return jnp.pad(val, widths)
 
 
 def unpack_tiles(tiles, num_tokens, num_chans):
@@ -58,6 +65,10 @@
     for shape_one in shapes[4:]:
         pieces.append(flat[start:start + shape_one[0]])
         start = start + shape_one[0]
+    pieces[0] = pad_tokens(pieces[0], 0, num_tokens)
+    pieces[1] = pad_tokens(pieces[1], 1, num_tokens)
+    pieces[2], pieces[3] = lax.optimization_barrier((pieces[2], pieces[3]))
+    pieces[7] = pad_tokens(pieces[7], 0, num_tokens)
     return pieces
 
 
@@ -512,18 +523,18 @@
     return layer_out, (x_in, normed, slope_tok, act_tok, after_tok, normed2, slope_ch, act_ch)
 
 
-def layer_backward(d_out, weights, cache, tag, flat_len):
-    num_tokens, num_chans = d_out.shape[1:]
+def layer_backward(d_out, weights, cache, tag, flat_len, num_tokens):
+    num_chans = d_out.shape[2]
     w_tok1, w_tok2, w_ch1, w_ch2, ln1_g, ln1_b, b_tok1, b_tok2, ln2_g, ln2_b, b_ch1, b_ch2 = weights
     x_in, normed, slope_tok, act_tok, after_tok, normed2, slope_ch, act_ch = cache
     d_out_bf = d_out.astype(jnp.bfloat16)
     g_b_ch2 = jnp.sum(d_out, axis=(0, 1))
-    tokens = d_out.shape[0] * num_tokens
+    tokens = d_out.shape[0] * d_out.shape[1]
     mat_tiles = [math.prod(shape_one) // LANES for shape_one in piece_shapes(num_tokens, num_chans)[:4]]
     row1 = mat_tiles[0] + mat_tiles[1]
     d_normed2, bias_rows, flat_grad = mlp_grad(
         d_out_bf.reshape(tokens, num_chans), act_ch.reshape(tokens, -1), slope_ch.reshape(tokens, -1), normed2.reshape(tokens, num_chans),
-        w_ch1, w_ch2, flat_len // LANES, row1, row1 + mat_tiles[2], tokens // 7)
+        w_ch1, w_ch2, flat_len // LANES, row1, row1 + mat_tiles[2], tokens // 5)
     g_b_ch1 = jnp.sum(bias_rows, axis=0)
     d_normed2 = d_normed2.reshape(d_out.shape)
     with jax.named_scope(tag + '_ln2'):
@@ -541,23 +552,22 @@
     d_normed = scoped(tag + '_dnt', 'bcj,sj->bsc', d_hid_tok_bf, w_tok1, preferred_element_type=jnp.float32)
     d_in_ln, g_ln1_g, g_ln1_b = norm_grad(x_in, ln1_g, ln1_b, d_normed)
     d_in = d_in_ln + d_after
-    vectors = jnp.concatenate([g_ln1_g, g_ln1_b, g_b_tok1, g_b_tok2, g_ln2_g, g_ln2_b, g_b_ch1, g_b_ch2])
+    vectors = jnp.concatenate([g_ln1_g, g_ln1_b, g_b_tok1, g_b_tok2[:num_tokens], g_ln2_g, g_ln2_b, g_b_ch1, g_b_ch2])
     last_row = row1 + mat_tiles[2] + mat_tiles[3]
     vectors = jnp.pad(vectors, (0, flat_len - last_row * LANES - vectors.shape[0])).reshape(-1, LANES)
-    tok_rows = jnp.concatenate([g_w_tok1.reshape(-1, LANES), g_w_tok2.reshape(-1, LANES)], axis=0)
+    tok_rows = jnp.concatenate([g_w_tok1[:num_tokens].reshape(-1, LANES), g_w_tok2[:, :num_tokens].reshape(-1, LANES)], axis=0)
     flat_grad = lax.dynamic_update_slice(flat_grad, tok_rows, (0, 0))
     flat_grad = lax.dynamic_update_slice(flat_grad, vectors, (last_row, 0))
     return d_in, flat_grad
 
 
-def head_step(hidden, labels, small_full, head_full, num_classes, global_b):
-    num_tokens = hidden.shape[1]
+def head_step(hidden, labels, small_full, head_full, num_classes, global_b, num_tokens):
     num_chans = hidden.shape[2]
     lnf_g = small_full[:num_chans]
     lnf_b = small_full[num_chans:2 * num_chans]
     head_b = small_full[2 * num_chans:2 * num_chans + num_classes]
     normed = layer_norm(hidden, lnf_g, lnf_b)
-    pooled = (jnp.sum(normed, axis=1, dtype=jnp.float32) / num_tokens).astype(jnp.bfloat16)
+    pooled = (jnp.sum(normed[:, :num_tokens], axis=1, dtype=jnp.float32) / num_tokens).astype(jnp.bfloat16)
     is_class = jnp.arange(HEAD_PAD)[None, :] < num_classes
     logits = jnp.dot(pooled, head_full, preferred_element_type=jnp.float32) + jnp.pad(head_b.astype(jnp.float32), (0, HEAD_PAD - num_classes))
     logits = jnp.where(is_class, logits, -jnp.inf)
@@ -570,7 +580,8 @@
     g_head_b = jnp.sum(d_logits, axis=0)[:num_classes]
     g_head_w = jnp.einsum('bc,bk->ck', pooled, d_logits_bf, preferred_element_type=jnp.float32)
     d_pooled = jnp.einsum('bk,ck->bc', d_logits_bf, head_full, preferred_element_type=jnp.float32)
-    d_normed = jnp.broadcast_to((d_pooled / num_tokens)[:, None, :], normed.shape)
+    is_token = jnp.arange(hidden.shape[1])[None, :, None] < num_tokens
+    d_normed = jnp.where(is_token, (d_pooled / num_tokens)[:, None, :], 0.0)
     d_hidden, g_lnf_g, g_lnf_b = norm_grad(hidden, lnf_g, lnf_b, d_normed)
     g_small = jnp.concatenate([g_lnf_g, g_lnf_b, g_head_b])
     return loss_sum, d_hidden, g_head_w, g_small
@@ -609,21 +620,21 @@
 
         weights = []
         caches = []
-        hidden = act_in
+        hidden = pad_tokens(act_in, 1, num_tokens)
         for layer_idx, flat in enumerate((flat0, flat1)):
             weights.append(unpack_tiles(flat.reshape(-1, ROWS, LANES), num_tokens, num_chans))
             hidden, cache = layer_forward(hidden, weights[layer_idx], f'f{layer_idx}')
             caches.append(cache)
         head_full = tiles_to_head(extra[:, :num_head], head_rows * GROUP)
         small_full = extra[:, num_head, 0].reshape(-1)
-        loss_sum, d_hidden, g_head_w, g_small = head_step(hidden, labels, small_full, head_full, num_classes, global_b)
+        loss_sum, d_hidden, g_head_w, g_small = head_step(hidden, labels, small_full, head_full, num_classes, global_b, num_tokens)
 
         head_blocks = head_to_tiles(g_head_w).reshape(GROUP, num_head, ROWS, LANES)
         g_small = jnp.pad(g_small, (0, small_len * GROUP - g_small.shape[0])).reshape(GROUP, 1, 1, small_len)
         small_blocks = jnp.pad(g_small, ((0, 0), (0, 0), (0, ROWS - 1), (0, 0)))
         packed = [None] * num_layers
         for layer_idx in reversed(range(num_layers)):
-            d_hidden, flat_grad = layer_backward(d_hidden, weights[layer_idx], caches[layer_idx], f'b{layer_idx}', flat_len)
+            d_hidden, flat_grad = layer_backward(d_hidden, weights[layer_idx], caches[layer_idx], f'b{layer_idx}', flat_len, num_tokens)
             packed[layer_idx] = flat_grad.reshape(flat0.shape)
         summed0, summed1 = scatter_grads(packed[0], packed[1], jnp.concatenate([head_blocks, small_blocks], axis=1), win_tiles)
         layer_g = jnp.stack([window_to_share(summed0, share_len), window_to_share(summed1[:win_tiles], share_len)])

time: 687 us -> 577 us (0.84)
  local copies, waits for them, and re-layouts: 160 us -> 60.4 us
  other arithmetic: 108 us -> 93.5 us
    reshape x12 -> x4, local copies, waits for them, and re-layouts: 85.4 us -> 4 us  [the longest x2 2.57 us: layer_backward(): g_w_tok1[:num_tokens].reshape(-1, LANES)]
    reshape x12 -> x10, local copies, waits for them, and re-layouts: 31.9 us -> 16.8 us  [unpack_tiles(): pieces.append(tiles[start:start + count].reshape(shape_one))]
    convert_element_type x2 -> x0, local copies, waits for them, and re-layouts: 10.4 us -> none  [layer_norm(): (normed * ln_gain.astype(jnp.float32) + ln_shift.astype(jnp.float32)).ast...]
    dot_general x2, matrix products: 24.6 us -> 15.7 us  [layer_forward(): jnp.einsum('bsd,dc->bsc', act_ch, w_ch2, preferred_element_type=jnp.float32)]
where the time goes in v2:
time: 577 us; the launch traced here: 566 us
  Pallas kernels  268 us (46%)
  matrix products  137 us (24%)
  other arithmetic  93.5 us (16%)
  local copies, waits for them, and re-layouts  60.4 us (10%)
  between operations  6.86 us (1%)
    pallas_call x1, Pallas kernels, scatter_grads(): pl.pallas_call(scatter_kernel, out_shape=tuple((jax.ShapeDtypeStruct((siz...  116 us
    pallas_call x2, Pallas kernels, mlp_grad(): pl.pallas_call(functools.partial(mlp_grad_kernel, row1=row1, row2=row2),...  88 us
    dot_general x10, matrix products, scoped(): return jnp.einsum(spec, lhs, rhs, **kwargs)  87.5 us
    pallas_call x1, Pallas kernels, gather_shares(): pl.pallas_call(gather_kernel, out_shape=(jax.ShapeDtypeStruct(flat, dtype...  55 us
    reduce_sum x7, other arithmetic, layer_norm(): normed * ln_gain.astype(jnp.float32) + ln_shift.astype(jnp.float32)  27.3 us
    dot_general x2, matrix products, layer_backward(): jnp.einsum('bsc,js->bcj', d_after_bf, w_tok2, preferred_element_type=jnp....  17.9 us
    reshape x10, local copies, waits for them, and re-layouts, unpack_tiles(): pieces.append(tiles[start:start + count].reshape(shape_one))  16.8 us
    dot_general x2, matrix products, layer_forward(): jnp.einsum('bsd,dc->bsc', act_ch, w_ch2, preferred_element_type=jnp.float32)  15.7 us

profile of v2, /device:TPU:0, one launch (start us, length us, event | category | flops | bytes accessed | tf_op | source)
XLA Modules:
  0.0 566.0 jit_solution(9742964603299314194)
XLA Ops:
  7.9 55.0 %gather_shares.1 = (bf16[8,269,8,128]{3,2,1,0:T(8,128)(2,1)}, bf16[8,269,8,128]{3,2,1,0:T(8,128)(2,1)}, bf16[32,17,8,128]{3,2,1,0:T(8,128)(2,1)}) custom-call(bf16[66,8,128]{2,1,0:T(8,128)(2,1)} %slice_bitcast_fusion.2.inner0_ref, bf16[66,8,128]{2,1,0:T(8,128)(2,1)} %slice_bitcast_fusion.1.inner1_ref, bf16[21,8,128]{2,1,0:T(8,128)(2,1)} %copy-done.45), custom_call_target="tpu_custom_call" | custom-call | tf_op jit(solution)/shard_map/gather_shares/pallas_call | solution.py:207
  79.0 5.8 %fusion.95 = f32[16,512,256]{2,1,0:T(8,128)} fusion(f32[512]{0:T(512)} %get-tuple-element.124, f32[512]{0:T(512)} %get-tuple-element.125, f32[16,200]{1,0:T(8,128)S(1)} %add_rsqrt_fusion, f32[16,200]{1,0:T(8,128)S(1)} %broadcast_multiply_fusion.4, bf16[16,196,512]{2,1,0:T(8,128)(2,1)S(1)} %copy.24, bf16[196,256]{1,0:T(8,128)(2,1)} %reshape.467), kind=kOutput, calls=%fused_computation.148 | convolution fusion | flops 848691200 | bytes 11729920 | tf_op jit(solution)/shard_map/f0_tok1/bsc,sj->bcj/dot_general | solution.py:506
  85.3 6.9 %convert_reduce_fusion.3 = (f32[16,200]{1,0:T(8,128)S(1)}, bf16[16,200,512]{2,1,0:T(8,128)(2,1)S(1)}) fusion(f32[200]{0:T(256)S(1)} %copy-done.74, f32[16,512,256]{2,1,0:T(8,128)} %fusion.95, f32[256]{0:T(256)S(1)} %slice_convert_fusion.15, bf16[256,196]{0,1:T(8,128)(2,1)S(1)} %copy.25, bf16[16,196,512]{2,1,0:T(8,128)(2,1)} %copy-done.9), kind=kOutput, calls=%fused_computation.29 | convolution fusion | flops 867562368 | bytes 14991648 | tf_op jit(solution)/shard_map/f0_tok2/bcj,js->bsc/dot_general | solution.py:515
  97.6 4.5 fusion.167
  102.1 4.1 reshape.468.w1_ref
  106.2 4.3 reshape.469.w2_ref
  110.6 23.5 %multiply_add_fusion = (f32[16,200,2048]{2,1,0:T(8,128)}, bf16[16,200,2048]{2,1,0:T(8,128)(2,1)S(1)}) fusion(f32[2048]{0:T(1024)S(1)} %slice_convert_fusion.1, bf16[16,200,512]{2,1,0:T(8,128)(2,1)} %fusion.49, bf16[512,2048]{1,0:T(8,128)(2,1)} %reshape.468.w1_ref), kind=kOutput, calls=%fused_computation | convolution fusion | flops 6822297600 | bytes 44703744 | tf_op jit(solution)/shard_map/f0_ch1/bsc,cd->bsd/dot_general | solution.py:506
  134.1 7.8 %convert_reduce_fusion.2 = (f32[16,200]{1,0:T(8,128)S(1)}, bf16[16,200,512]{2,1,0:T(8,128)(2,1)S(1)}) fusion(f32[512]{0:T(512)S(1)} %copy-done.63, bf16[16,200,2048]{2,1,0:T(8,128)(2,1)S(1)} %get-tuple-element.103, bf16[2048,512]{1,0:T(8,128)(2,1)S(1)} %copy-done.17, bf16[16,200,512]{2,1,0:T(8,128)(2,1)S(1)} %get-tuple-element.131), kind=kOutput, calls=%fused_computation.22 | convolution fusion | flops 6720713728 | bytes 21772800 | tf_op jit(solution)/shard_map/f0_ch2/bsd,dc->bsc/dot_general | solution.py:521
  146.6 8.0 %fusion.92 = f32[16,512,256]{2,1,0:T(8,128)} fusion(bf16[16,200,512]{2,1,0:T(8,128)(2,1)} %copy-done.5, f32[512]{0:T(512)S(1)} %copy-done.59, f32[512]{0:T(512)S(1)} %get-tuple-element.120, f32[16,200]{1,0:T(8,128)S(1)} %fusion.136, f32[16,200]{1,0:T(8,128)S(1)} %broadcast_multiply_fusion.2, bf16[196,256]{1,0:T(8,128)(2,1)S(1)} %reshape.473), kind=kOutput, calls=%fused_computation.147 | convolution fusion | flops 848691200 | bytes 11795456 | tf_op jit(solution)/shard_map/f1_tok1/bsc,sj->bcj/dot_general | solution.py:506
  155.8 7.4 %convert_reduce_fusion.1 = (f32[16,200]{1,0:T(8,128)S(1)}, bf16[16,200,512]{2,1,0:T(8,128)(2,1)S(1)}) fusion(f32[200]{0:T(256)} %pad_convert_fusion.1, f32[16,512,256]{2,1,0:T(8,128)} %fusion.92, f32[256]{0:T(256)S(1)} %slice_convert_fusion.14, bf16[256,196]{0,1:T(8,128)(2,1)S(1)} %copy.26, bf16[16,200,512]{2,1,0:T(8,128)(2,1)S(1)} %copy-done.6), kind=kOutput, calls=%fused_computation.15 | convolution fusion | flops 867562368 | bytes 15057184 | tf_op jit(solution)/shard_map/f1_tok2/bcj,js->bsc/dot_general | solution.py:515
  167.5 3.9 fusion.165
  171.3 4.2 reshape.474.w1_ref
  178.0 23.5 %multiply_add_fusion.1 = (f32[16,200,2048]{2,1,0:T(8,128)}, bf16[16,200,2048]{2,1,0:T(8,128)(2,1)S(1)}) fusion(f32[2048]{0:T(1024)S(1)} %copy-done.55, bf16[16,200,512]{2,1,0:T(8,128)(2,1)} %fusion.42, bf16[512,2048]{1,0:T(8,128)(2,1)} %reshape.474.w1_ref), kind=kOutput, calls=%fused_computation.1 | convolution fusion | flops 6822297600 | bytes 44703744 | tf_op jit(solution)/shard_map/f1_ch1/bsc,cd->bsd/dot_general | solution.py:506
  201.5 7.8 %convert_reduce_fusion.8 = (f32[16,200]{1,0:T(8,128)S(1)}, bf16[16,200,512]{2,1,0:T(8,128)(2,1)S(1)}) fusion(f32[512]{0:T(512)S(1)} %copy-done.62, bf16[16,200,2048]{2,1,0:T(8,128)(2,1)S(1)} %get-tuple-element.105, bf16[2048,512]{1,0:T(8,128)(2,1)S(1)} %copy-done.18, bf16[16,200,512]{2,1,0:T(8,128)(2,1)S(1)} %copy-done.1), kind=kOutput, calls=%fused_computation.56 | convolution fusion | flops 6720713728 | bytes 21772800 | tf_op jit(solution)/shard_map/f1_ch2/bsd,dc->bsc/dot_general | solution.py:521
  216.8 4.5 fusion.72
  223.1 4.0 fusion.57
  227.1 43.8 %mlp_grad.2 = (bf16[3200,512]{1,0:T(8,128)(2,1)}, f32[8,2048]{1,0:T(8,128)}, f32[17216,128]{1,0:T(8,128)}) custom-call(bf16[3200,512]{1,0:T(8,128)(2,1)} %bitcast.226, bf16[3200,2048]{1,0:T(8,128)(2,1)} %bitcast.257, f32[3200,2048]{1,0:T(8,128)} %bitcast.255, bf16[3200,512]{1,0:T(8,128)(2,1)} %bitcast.228, bf16[512,2048]{1,0:T(8,128)(2,1)} %reshape.474.w1_ref, ...), custom_call_target="tpu_custom_call" | custom-call | flops 26843545600 | bytes 61734912 | tf_op jit(solution)/shard_map/mlp_grad/pallas_call | solution.py:412
  271.0 4.6 convert_reduce_fusion.11
  276.3 5.3 fusion.43
  283.3 6.2 %convert_reduce_fusion.7 = (f32[512]{0:T(512)}, f32[200]{0:T(256)}, bf16[16,200,512]{2,1,0:T(8,128)(2,1)S(1)}) fusion(f32[16,200]{1,0:T(8,128)S(1)} %add_multiply_fusion.4, f32[16,200]{1,0:T(8,128)S(1)} %multiply_multiply_fusion.4, f32[16,200]{1,0:T(8,128)S(1)} %broadcast_multiply_fusion.1, bf16[16,200,512]{2,1,0:T(8,128)(2,1)S(1)} %copy-done.2, ...), kind=kLoop, calls=%fused_computation.53 | loop fusion | flops 37682488 | bytes 16509928 | tf_op jit(solution)/shard_map/reduce_sum | solution.py:531
  289.6 7.0 %fusion.173 = (f32[256]{0:T(256)}, bf16[16,512,256]{2,1,0:T(8,128)(2,1)S(1)}) fusion(f32[16,512,256]{2,1,0:T(8,128)S(1)} %bitcast.261, f32[256]{0:T(256)S(1)} %copy-done.73, bf16[256,196]{0,1:T(8,128)(2,1)S(1)} %copy-done.32, bf16[16,200,512]{2,1,0:T(8,128)(2,1)S(1)} %copy-done.14, bf16[16,200,512]{2,1,0:T(8,128)(2,1)S(1)} %get-tuple-element.96), kind=kOutput, calls=%fused_computation.298 | convolution fusion | flops 887357184 | bytes 19238912 | tf_op jit(solution)/shard_map/b1_dtok/bsc,js->bcj/dot_general | solution.py:547
  296.6 4.5 fusion.61
  302.7 6.5 %fusion.164 = (bf16[16,200,512]{2,1,0:T(8,128)(2,1)}, f32[16,200,512]{2,1,0:T(8,128)}) fusion(bf16[16,200,512]{2,1,0:T(8,128)(2,1)S(1)} %get-tuple-element.96, f32[16,200]{1,0:T(8,128)S(1)} %add_multiply_fusion.3, f32[16,200]{1,0:T(8,128)S(1)} %multiply_multiply_fusion.3, f32[16,200]{1,0:T(8,128)S(1)} %broadcast_multiply_fusion.2, ...), kind=kLoop, calls=%fused_computation.289 | loop fusion | flops 40960000 | bytes 23060680 | tf_op jit(solution)/shard_map/convert_element_type | solution.py:530
  309.2 44.1 %mlp_grad.3 = (bf16[3200,512]{1,0:T(8,128)(2,1)}, f32[8,2048]{1,0:T(8,128)}, f32[17216,128]{1,0:T(8,128)}) custom-call(bf16[3200,512]{1,0:T(8,128)(2,1)} %bitcast.225, bf16[3200,2048]{1,0:T(8,128)(2,1)} %bitcast.256, f32[3200,2048]{1,0:T(8,128)} %bitcast.254, bf16[3200,512]{1,0:T(8,128)(2,1)} %bitcast.227, bf16[512,2048]{1,0:T(8,128)(2,1)} %reshape.468.w1_ref, ...), custom_call_target="tpu_custom_call" | custom-call | flops 26843545600 | bytes 61734912 | tf_op jit(solution)/shard_map/mlp_grad/pallas_call | solution.py:412
  353.5 4.0 convert_reduce_fusion.10
  357.6 6.1 %fusion.50 = (f32[512]{0:T(512)S(1)}, f32[16,200]{1,0:T(8,128)S(1)}, f32[16,200,512]{2,1,0:T(8,128)S(1)}) fusion(bf16[16,200,512]{2,1,0:T(8,128)(2,1)S(1)} %copy-done.4, f32[16,200]{1,0:T(8,128)S(1)} %copy-done.24, f32[16,200]{1,0:T(8,128)S(1)} %copy-done.20, f32[512]{0:T(512)S(1)} %copy-done.44, bf16[16,200,512]{2,1,0:T(8,128)(2,1)} %bitcast.212), kind=kLoop, calls=%fused_computation.93 | loop fusion | flops 14741888 | bytes 13149696 | tf_op jit(solution)/shard_map/b0_ln2/transpose(jvp())/reduce_sum | solution.py:486
  365.5 3.8 fusion.157
  373.0 10.9 %fusion.172 = (f32[256]{0:T(256)}, bf16[16,512,256]{2,1,0:T(8,128)(2,1)S(1)}) fusion(f32[16,512,256]{2,1,0:T(8,128)} %fusion.95, f32[256]{0:T(256)} %copy-done.70, bf16[256,196]{0,1:T(8,128)(2,1)} %copy-done.30, f32[16,200,512]{2,1,0:T(8,128)} %get-tuple-element.100, bf16[16,200,512]{2,1,0:T(8,128)(2,1)} %copy-done.15), kind=kOutput, calls=%fused_computation.297 | convolution fusion | flops 885718784 | bytes 22515712 | tf_op jit(solution)/shard_map/b0_dtok/bsc,js->bcj/dot_general | solution.py:547
  394.5 8.6 %fusion.100 = f32[256,200]{0,1:T(8,128)S(1)} fusion(bf16[16,200,512]{2,1,0:T(8,128)(2,1)} %fusion.57, bf16[16,200,512]{2,1,0:T(8,128)(2,1)} %copy-done.11, f32[16,512,256]{2,1,0:T(8,128)} %fusion.92, f32[256]{0:T(256)} %copy-done.72), kind=kOutput, calls=%fused_computation.150 | convolution fusion | flops 864288768 | bytes 15148032 | tf_op jit(solution)/shard_map/b1_gt2/bcj,bsc->js/dot_general | solution.py:506
  405.2 4.5 fusion.103
  419.6 115.5 %scatter_grads.1 = (f32[68,8,128]{2,1,0:T(8,128)}, f32[85,8,128]{2,1,0:T(8,128)}) custom-call(f32[8,269,8,128]{3,2,1,0:T(8,128)} %bitcast.217, f32[8,269,8,128]{3,2,1,0:T(8,128)} %bitcast.216, f32[32,17,8,128]{3,2,1,0:T(8,128)} %select_maximum_fusion.extra_ref), custom_call_target="tpu_custom_call" | custom-call | tf_op jit(solution)/shard_map/scatter_grads/pallas_call | solution.py:336
  547.0 9.3 %sum_over_devices.1 = f32[8,128]{1,0:T(8,128)} custom-call(f32[8,128]{1,0:T(8,128)} %scatter.9.x_ref), custom_call_target="tpu_custom_call" | custom-call | tf_op jit(solution)/shard_map/sum_over_devices/pallas_call | solution.py:464
  (299 shorter events, 99.2 us)
Async XLA Ops:
  68.1 78.5 %copy-start.50 = (f32[512]{0:T(512)}, f32[512]{0:T(512)S(1)}, u32[]{:S(2)}) copy-start(f32[512]{0:T(512)S(1)} %get-tuple-element.120) | copy-start | bytes 6148
  70.7 23.7 %copy-start.43 = (f32[512]{0:T(512)}, f32[512]{0:T(512)S(1)}, u32[]{:S(2)}) copy-start(f32[512]{0:T(512)S(1)} %get-tuple-element.121) | copy-start | bytes 6148
  92.3 41.8 %copy-start.3 = (bf16[16,200,512]{2,1,0:T(8,128)(2,1)}, bf16[16,200,512]{2,1,0:T(8,128)(2,1)S(1)}, u32[]{:S(2)}) copy-start(bf16[16,200,512]{2,1,0:T(8,128)(2,1)S(1)} %get-tuple-element.131) | copy-start | bytes 9830404
  110.6 23.5 %copy-start.17 = (bf16[2048,512]{1,0:T(8,128)(2,1)S(1)}, bf16[2048,512]{1,0:T(8,128)(2,1)}, u32[]{:S(2)}) copy-start(bf16[2048,512]{1,0:T(8,128)(2,1)} %reshape.469.w2_ref) | copy-start | bytes 6291460
  110.6 23.5 %copy-start.63 = (f32[512]{0:T(512)S(1)}, f32[512]{0:T(512)}, u32[]{:S(2)}) copy-start(f32[512]{0:T(512)} %get-tuple-element.122) | copy-start | bytes 6148
  134.1 12.5 %copy-start.59 = (f32[512]{0:T(512)S(1)}, f32[512]{0:T(512)}, u32[]{:S(2)}) copy-start(f32[512]{0:T(512)} %get-tuple-element.119) | copy-start | bytes 6148
  143.7 159.1 %copy-start.26 = (f32[16,200]{1,0:T(8,128)}, f32[16,200]{1,0:T(8,128)S(1)}, u32[]{:S(2)}) copy-start(f32[16,200]{1,0:T(8,128)S(1)} %broadcast_multiply_fusion.2) | copy-start | bytes 38404
  178.0 23.5 %copy-start.1 = (bf16[16,200,512]{2,1,0:T(8,128)(2,1)S(1)}, bf16[16,200,512]{2,1,0:T(8,128)(2,1)}, u32[]{:S(2)}) copy-start(bf16[16,200,512]{2,1,0:T(8,128)(2,1)} %copy-done) | copy-start | bytes 9830404
  178.0 23.5 %copy-start.18 = (bf16[2048,512]{1,0:T(8,128)(2,1)S(1)}, bf16[2048,512]{1,0:T(8,128)(2,1)}, u32[]{:S(2)}) copy-start(bf16[2048,512]{1,0:T(8,128)(2,1)} %reshape.475.w2_ref) | copy-start | bytes 6291460
  178.0 23.5 %copy-start.62 = (f32[512]{0:T(512)S(1)}, f32[512]{0:T(512)}, u32[]{:S(2)}) copy-start(f32[512]{0:T(512)} %get-tuple-element.117) | copy-start | bytes 6148
  276.3 13.2 %slice-start.4 = ((s8[8388608]{0:T(1024)(128)(4,1)}), s8[4194304]{0:T(1024)(128)(4,1)S(1)}, s32[]{:S(2)}) async-start(s8[8388608]{0:T(1024)(128)(4,1)} %bitcast.260), calls=%async_computation.4 | async-start | bytes 8388608
  289.5 13.2 %copy-start.11 = (bf16[16,200,512]{2,1,0:T(8,128)(2,1)}, bf16[16,200,512]{2,1,0:T(8,128)(2,1)S(1)}, u32[]{:S(2)}) copy-start(bf16[16,200,512]{2,1,0:T(8,128)(2,1)S(1)} %get-tuple-element.96) | copy-start | bytes 9830404
  309.2 44.2 %copy-start.24 = (f32[16,200]{1,0:T(8,128)S(1)}, f32[16,200]{1,0:T(8,128)}, u32[]{:S(2)}) copy-start(f32[16,200]{1,0:T(8,128)} %copy-done.23) | copy-start | bytes 38404
  309.2 44.3 %copy-start.44 = (f32[512]{0:T(512)S(1)}, f32[512]{0:T(512)}, u32[]{:S(2)}) copy-start(f32[512]{0:T(512)} %copy-done.43) | copy-start | bytes 6148
  309.2 48.4 %copy-start.4 = (bf16[16,200,512]{2,1,0:T(8,128)(2,1)S(1)}, bf16[16,200,512]{2,1,0:T(8,128)(2,1)}, u32[]{:S(2)}) copy-start(bf16[16,200,512]{2,1,0:T(8,128)(2,1)} %copy-done.3) | copy-start | bytes 9830404
  309.2 48.4 %copy-start.20 = (f32[16,200]{1,0:T(8,128)S(1)}, f32[16,200]{1,0:T(8,128)}, u32[]{:S(2)}) copy-start(f32[16,200]{1,0:T(8,128)} %copy-done.19) | copy-start | bytes 38404
  357.6 11.7 %slice-start.2 = ((s8[8388608]{0:T(1024)(128)(4,1)}), s8[4194304]{0:T(1024)(128)(4,1)S(1)}, s32[]{:S(2)}) async-start(s8[8388608]{0:T(1024)(128)(4,1)} %bitcast.258), calls=%async_computation.2 | async-start | bytes 8388608
  372.9 11.0 %copy-start.10 = (bf16[16,196,512]{2,1,0:T(8,128)(2,1)S(1)}, bf16[16,196,512]{2,1,0:T(8,128)(2,1)}, u32[]{:S(2)}) copy-start(bf16[16,196,512]{2,1,0:T(8,128)(2,1)} %copy-done.9) | copy-start | bytes 9633796
  373.0 10.9 %copy-start.36 = (f32[16,200]{1,0:T(8,128)S(1)}, f32[16,200]{1,0:T(8,128)}, u32[]{:S(2)}) copy-start(f32[16,200]{1,0:T(8,128)} %copy-done.35) | copy-start | bytes 38404
  373.0 10.9 %copy-start.49 = (f32[16,200]{1,0:T(8,128)S(1)}, f32[16,200]{1,0:T(8,128)}, u32[]{:S(2)}) copy-start(f32[16,200]{1,0:T(8,128)} %copy-done.48) | copy-start | bytes 38404
  373.0 10.9 %copy-start.60 = (f32[512]{0:T(512)S(1)}, f32[512]{0:T(512)}, u32[]{:S(2)}) copy-start(f32[512]{0:T(512)} %get-tuple-element.124) | copy-start | bytes 6148
  373.0 10.9 %copy-start.61 = (f32[512]{0:T(512)S(1)}, f32[512]{0:T(512)}, u32[]{:S(2)}) copy-start(f32[512]{0:T(512)} %get-tuple-element.125) | copy-start | bytes 6148
  405.2 11.0 %copy-start.53 = (f32[512]{0:T(512)S(1)}, f32[512]{0:T(512)}, u32[]{:S(2)}) copy-start(f32[512]{0:T(512)} %get-tuple-element.72) | copy-start | bytes 6148
  419.6 139.4 %copy-start.16 = (f32[2,68864]{1,0:T(2,128)S(1)}, f32[2,68864]{1,0:T(2,128)}, u32[]{:S(2)}) copy-start(f32[2,68864]{1,0:T(2,128)} %param.17) | copy-start | bytes 1652740
  419.6 139.4 %copy-start.21 = (f32[2,68864]{1,0:T(2,128)S(1)}, f32[2,68864]{1,0:T(2,128)}, u32[]{:S(2)}) copy-start(f32[2,68864]{1,0:T(2,128)} %param.20) | copy-start | bytes 1652740
  419.6 139.4 %copy-start.22 = (f32[2,68864]{1,0:T(2,128)S(1)}, f32[2,68864]{1,0:T(2,128)}, u32[]{:S(2)}) copy-start(f32[2,68864]{1,0:T(2,128)} %param.23) | copy-start | bytes 1652740
  535.2 27.3 %copy-start.27 = (f32[16,1000]{1,0:T(8,128)S(1)}, f32[16,1000]{1,0:T(8,128)}, u32[]{:S(2)}) copy-start(f32[16,1000]{1,0:T(8,128)} %param.18) | copy-start | bytes 192004
  535.2 27.3 %copy-start.41 = (f32[16,1000]{1,0:T(8,128)S(1)}, f32[16,1000]{1,0:T(8,128)}, u32[]{:S(2)}) copy-start(f32[16,1000]{1,0:T(8,128)} %param.21) | copy-start | bytes 192004
  535.2 27.3 %copy-start.42 = (f32[16,1000]{1,0:T(8,128)S(1)}, f32[16,1000]{1,0:T(8,128)}, u32[]{:S(2)}) copy-start(f32[16,1000]{1,0:T(8,128)} %param.24) | copy-start | bytes 192004
  535.2 28.0 %copy-start.65 = (f32[128]{0:T(128)S(1)}, f32[128]{0:T(128)}, u32[]{:S(2)}) copy-start(f32[128]{0:T(128)} %param.19) | copy-start | bytes 1540
  535.2 28.0 %copy-start.66 = (f32[128]{0:T(128)S(1)}, f32[128]{0:T(128)}, u32[]{:S(2)}) copy-start(f32[128]{0:T(128)} %param.22) | copy-start | bytes 1540
  535.2 28.0 %copy-start.67 = (f32[128]{0:T(128)S(1)}, f32[128]{0:T(128)}, u32[]{:S(2)}) copy-start(f32[128]{0:T(128)} %param.25) | copy-start | bytes 1540
  (51 other events, 296.9 us)

commit v3 on v2

--- a/solution.py
+++ b/solution.py
@@ -58,7 +58,7 @@
     shapes = piece_shapes(num_tokens, num_chans)
     for shape_one in shapes[:4]:
         count = math.prod(shape_one) // TILE
-        pieces.append(tiles[start:start + count].reshape(shape_one))
+        pieces.append(tiles[start:start + count].reshape(shape_one) if len(pieces) < 2 else None)
         start = start + count
     flat = tiles[start:].reshape(-1)
     start = 0
@@ -67,7 +67,8 @@
         start = start + shape_one[0]
     pieces[0] = pad_tokens(pieces[0], 0, num_tokens)
     pieces[1] = pad_tokens(pieces[1], 1, num_tokens)
-    pieces[2], pieces[3] = lax.optimization_barrier((pieces[2], pieces[3]))
+    tile1 = 2 * math.prod(shapes[0]) // TILE
+    pieces[2], pieces[3] = unpack_mats(tiles, shapes[2], shapes[3], tile1, tile1 + math.prod(shapes[2]) // TILE)
     pieces[7] = pad_tokens(pieces[7], 0, num_tokens)
     return pieces
 
@@ -106,6 +107,13 @@
 
     def device(self, rel):
         return self.split(rel)[0]
+
+
+def meet_all(me):
+    barrier = pltpu.get_barrier_semaphore()
+    for step in range(1, GROUP):
+        pl.semaphore_signal(barrier, inc=1, device_id=(lax.rem(me + step, GROUP),), device_id_type=pl.DeviceIdType.MESH)
+    pl.semaphore_wait(barrier, GROUP - 1)
 
 
 def meet_partners(peers):
@@ -221,9 +229,10 @@
     )(window0[1:-1], window1[1:-1], misc)
 
 
-def scatter_kernel(grad0_ref, grad1_ref, extra_ref, out0_ref, out1_ref, own0, own1, core0, core1, first0, first1, second0, second1, far0, far1,
-                   load_sems, send_sems, core_sems, first_sems, second_sems, far_sems):
-    peers = Peers(lax.axis_index(AXIS))
+def scatter_kernel(grad0_ref, grad1_ref, extra_ref, loss_ref, out0_ref, out1_ref, sums_ref, own0, own1, core0, core1, first0, first1, second0, second1, far0, far1,
+                   partial, held, load_sems, send_sems, core_sems, first_sems, second_sems, far_sems, sum_load_sem, sum_send_sems, sum_recv_sems, *, share_rows):
+    me = lax.axis_index(AXIS)
+    peers = Peers(me)
     num_tiles = out0_ref.shape[0]
     num_extra = extra_ref.shape[1]
     own, near, first_in, second_in, far_in = (own0, own1), (core0, core1), (first0, first1), (second0, second1), (far0, far1)
@@ -262,7 +271,9 @@
             for part in range(3):
                 loads[part, pos] = pltpu.make_async_copy(source(part, rel), slot(part, own, pos), load_sems.at[part, pos])
                 loads[part, pos].start()
-    meet_partners(peers)
+    loss_copy = pltpu.make_async_copy(loss_ref, partial.at[1], sum_load_sem.at[0])
+    loss_copy.start()
+    meet_all(me)
     for dist in dists:
         for pos, rel in targets(dist):
             for part in range(3):
@@ -320,11 +331,41 @@
             expect(far_in[side].at[dist - 1], send_sems.at[3 + side, 12 + dist], far_sems.at[side, dist - 1])
             total = total + far_in[side][dist - 1]
         (out0_ref, out1_ref)[side][...] = total
+
+    first_row = 2 * peers.split(0)[2] if share_rows % ROWS == 2 else lax.rem(share_rows * me, ROWS)
+    row = lax.broadcasted_iota(jnp.int32, (ROWS, LANES), 0)
+    squares = jnp.zeros((ROWS, LANES), jnp.float32)
+    for out_ref in (out0_ref, out1_ref):
+        head = jnp.where(row >= first_row, out_ref[0], 0.0)
+        tail = jnp.where(row < first_row + share_rows % ROWS, out_ref[num_tiles - 1], 0.0)
+        inner = out_ref[1:num_tiles - 1]
+        squares = squares + head * head + tail * tail + jnp.sum(inner * inner, axis=0)
+    rest = out1_ref[num_tiles:]
+    partial[0] = squares + jnp.sum(rest * rest, axis=0)
     for copy in sends:
         copy.wait_send()
-
-
-def scatter_grads(grad0, grad1, extra, num_tiles):
+    loss_copy.wait()
+    mine = pltpu.make_async_copy(partial, held.at[me], sum_load_sem.at[1])
+    mine.start()
+    posts = []
+    for step in range(1, GROUP):
+        copy = pltpu.make_async_remote_copy(
+            src_ref=partial, dst_ref=held.at[me], send_sem=sum_send_sems.at[step], recv_sem=sum_recv_sems.at[me],
+            device_id=(lax.rem(me + step, GROUP),), device_id_type=pl.DeviceIdType.MESH)
+        copy.start()
+        posts.append(copy)
+    mine.wait()
+    for step in range(1, GROUP):
+        peer = lax.rem(me + step, GROUP)
+        pltpu.make_async_remote_copy(
+            src_ref=partial, dst_ref=held.at[peer], send_sem=sum_send_sems.at[step], recv_sem=sum_recv_sems.at[peer],
+            device_id=(peer,), device_id_type=pl.DeviceIdType.MESH).wait_recv()
+    for copy in posts:
+        copy.wait_send()
+    sums_ref[...] = jnp.sum(held[...], axis=0)
+
+
+def scatter_grads(grad0, grad1, extra, loss_tile, num_tiles, share_rows):
     num_extra = extra.shape[1]
     sizes = (num_tiles, num_tiles + num_extra)
     vmem = pl.BlockSpec(memory_space=pltpu.VMEM)
@@ -334,21 +375,26 @@
         return [pltpu.VMEM((count, size, ROWS, LANES), jnp.float32) for size in sizes]
 
     return pl.pallas_call(
-        scatter_kernel,
-        out_shape=tuple(jax.ShapeDtypeStruct((size, ROWS, LANES), jnp.float32) for size in sizes),
-        in_specs=[hbm] * 3,
-        out_specs=(vmem, vmem),
+        functools.partial(scatter_kernel, share_rows=share_rows),
+        out_shape=tuple(jax.ShapeDtypeStruct((size, ROWS, LANES), jnp.float32) for size in sizes + (2,)),
+        in_specs=[hbm] * 3 + [vmem],
+        out_specs=(vmem, vmem, vmem),
         scratch_shapes=buffers(16) + buffers(16) + buffers(8) + buffers(4) + buffers(3) + [
+            pltpu.VMEM((2, ROWS, LANES), jnp.float32),
+            pltpu.VMEM((GROUP, 2, ROWS, LANES), jnp.float32),
             pltpu.SemaphoreType.DMA((3, 16)),
             pltpu.SemaphoreType.DMA((5, 16)),
             pltpu.SemaphoreType.DMA((3, 16)),
             pltpu.SemaphoreType.DMA((2, 8)),
             pltpu.SemaphoreType.DMA((2, 4)),
             pltpu.SemaphoreType.DMA((2, 3)),
+            pltpu.SemaphoreType.DMA((2,)),
+            pltpu.SemaphoreType.DMA((GROUP,)),
+            pltpu.SemaphoreType.DMA((GROUP,)),
         ],
         compiler_params=pltpu.CompilerParams(collective_id=2, has_side_effects=True),
         name='scatter_grads',
-    )(grad0, grad1, extra)
+    )(grad0, grad1, extra, loss_tile)
 
 
 NT_DIMS = (((1,), (1,)), ((), ()))
@@ -431,51 +477,45 @@
     )(d_out, act, slope, normed, w1, w2)
 
 
-def sum_kernel(x_ref, out_ref, held, local_sem, send_sems, recv_sems):
-    me = lax.axis_index(AXIS)
-    barrier = pltpu.get_barrier_semaphore()
-    for step in range(1, GROUP):
-        pl.semaphore_signal(barrier, inc=1, device_id=((me + step) % GROUP,), device_id_type=pl.DeviceIdType.MESH)
-    own = pltpu.make_async_copy(x_ref, held.at[me], local_sem)
-    own.start()
-    pl.semaphore_wait(barrier, GROUP - 1)
-    sends = []
-    for step in range(1, GROUP):
-        copy = pltpu.make_async_remote_copy(
-            src_ref=x_ref, dst_ref=held.at[me], send_sem=send_sems.at[step], recv_sem=recv_sems.at[me],
-            device_id=((me + step) % GROUP,), device_id_type=pl.DeviceIdType.MESH)
-        copy.start()
-        sends.append(copy)
-    own.wait()
-    for step in range(1, GROUP):
-        peer = (me + step) % GROUP
-        pltpu.make_async_remote_copy(
-            src_ref=x_ref, dst_ref=held.at[peer], send_sem=send_sems.at[step], recv_sem=recv_sems.at[peer],
-            device_id=(peer,), device_id_type=pl.DeviceIdType.MESH).wait_recv()
-    for copy in sends:
-        copy.wait_send()
-    out_ref[...] = jnp.sum(held[...], axis=0)
-
-
-def sum_over_devices(values):
-    block = jnp.zeros((ROWS, LANES), jnp.float32)
-    for pos, value in enumerate(values):
-        block = block.at[0, pos].set(value)
-    total = pl.pallas_call(
-        sum_kernel,
-        out_shape=jax.ShapeDtypeStruct((ROWS, LANES), jnp.float32),
-        in_specs=[pl.BlockSpec(memory_space=pltpu.VMEM)],
-        out_specs=pl.BlockSpec(memory_space=pltpu.VMEM),
+CHUNK_TILES = 128
+
+
+def unpack_kernel(flat_ref, w1_ref, w2_ref, raw, spread, sems, *, tile1, tile2):
+    chans, hid = w1_ref.shape
+    num_chunks = chans * hid // (CHUNK_TILES * TILE)
+    copies = []
+    for mat, first in enumerate((tile1, tile2)):
+        for chunk in range(num_chunks):
+            pos = mat * num_chunks + chunk
+            copies.append(pltpu.make_async_copy(flat_ref.at[pl.ds(first + chunk * CHUNK_TILES, CHUNK_TILES)], raw.at[pos], sems.at[pos]))
+            copies[-1].start()
+    for mat, out_ref in enumerate((w1_ref, w2_ref)):
+        wide = out_ref.shape[1] // LANES
+        count = CHUNK_TILES * ROWS // wide
+        for chunk in range(num_chunks):
+            pos = mat * num_chunks + chunk
+            copies[pos].wait()
+            spread[pos % 2] = raw[pos].astype(jnp.float32).reshape(CHUNK_TILES * ROWS, LANES)
+            for col in range(wide):
+                out_ref[chunk * count:(chunk + 1) * count, col * LANES:(col + 1) * LANES] = spread[pos % 2, pl.ds(col, count, stride=wide), :].astype(out_ref.dtype)
+
+
+def unpack_mats(flat, shape1, shape2, tile1, tile2):
+    vmem = pl.BlockSpec(memory_space=pltpu.VMEM)
+    num_chunks = math.prod(shape1) // (CHUNK_TILES * TILE)
+    return pl.pallas_call(
+        functools.partial(unpack_kernel, tile1=tile1, tile2=tile2),
+        out_shape=(jax.ShapeDtypeStruct(shape1, flat.dtype), jax.ShapeDtypeStruct(shape2, flat.dtype)),
+        in_specs=[pl.BlockSpec(memory_space=pl.ANY)],
+        out_specs=(vmem, vmem),
         scratch_shapes=[
-            pltpu.VMEM((GROUP, ROWS, LANES), jnp.float32),
-            pltpu.SemaphoreType.DMA,
-            pltpu.SemaphoreType.DMA((GROUP,)),
-            pltpu.SemaphoreType.DMA((GROUP,)),
+            pltpu.VMEM((2 * num_chunks, CHUNK_TILES, ROWS, LANES), flat.dtype),
+            pltpu.VMEM((2, CHUNK_TILES * ROWS, LANES), jnp.float32),
+            pltpu.SemaphoreType.DMA((2 * num_chunks,)),
         ],
-        compiler_params=pltpu.CompilerParams(collective_id=0, has_side_effects=True),
-        name='sum_over_devices',
-    )(block)
-    return [total[0, pos] for pos in range(len(values))]
+        cost_estimate=pl.CostEstimate(flops=0, bytes_accessed=8 * math.prod(shape1), transcendentals=0),
+        name='unpack_mats',
+    )(flat)
 
 
 def layer_norm(x_in, ln_gain, ln_shift):
@@ -636,13 +676,14 @@
         for layer_idx in reversed(range(num_layers)):
             d_hidden, flat_grad = layer_backward(d_hidden, weights[layer_idx], caches[layer_idx], f'b{layer_idx}', flat_len, num_tokens)
             packed[layer_idx] = flat_grad.reshape(flat0.shape)
-        summed0, summed1 = scatter_grads(packed[0], packed[1], jnp.concatenate([head_blocks, small_blocks], axis=1), win_tiles)
+        loss_tile = jnp.pad(loss_sum.reshape(1, 1), ((0, ROWS - 1), (0, LANES - 1)))
+        extra_blocks = jnp.concatenate([head_blocks, small_blocks], axis=1)
+        summed0, summed1, sums = scatter_grads(packed[0], packed[1], extra_blocks, loss_tile, win_tiles, share_len // LANES)
         layer_g = jnp.stack([window_to_share(summed0, share_len), window_to_share(summed1[:win_tiles], share_len)])
         head_g = tiles_to_head(summed1[win_tiles:win_tiles + num_head], head_rows)[:, :num_classes]
         small_g = summed1[win_tiles + num_head, 0]
 
-        sq_local = jnp.sum(jnp.square(layer_g)) + jnp.sum(jnp.square(head_g)) + jnp.sum(jnp.square(small_g))
-        loss_total, sq_total = sum_over_devices([loss_sum, sq_local])
+        sq_total, loss_total = jnp.sum(sums[0]), jnp.sum(sums[1])
         loss_value = loss_total / global_b
         clip_scale = 1.0 / jnp.maximum(1.0, jnp.sqrt(sq_total))
         flat_pos = lax.axis_index(AXIS) * share_len + jnp.arange(share_len)

time: 577 us -> 550 us (0.953)
  local copies, waits for them, and re-layouts: 60.4 us -> 29.4 us
  Pallas kernels: 268 us -> 278 us
    reshape x10 -> x6, local copies, waits for them, and re-layouts: 16.8 us -> 1.69 us  [unpack_tiles(): tiles[start:start + count].reshape(shape_one)]
    pallas_call x2 -> x3, Pallas kernels: 125 us -> 135 us  [the longest x1 124 us: scatter_grads(): pl.pallas_call(functools.partial(scatter_kernel, share_rows=share_rows),...]
    slice x5 -> x2, local copies, waits for them, and re-layouts: 11.6 us -> 1.92 us  [unpack_tiles(): tiles[start:start + count].reshape(shape_one)]
where the time goes in v3:
time: 550 us; the launch traced here: 540 us
  Pallas kernels  278 us (51%)
  matrix products  138 us (25%)
  other arithmetic  90 us (16%)
  local copies, waits for them, and re-layouts  29.4 us (5%)
    pallas_call x1, Pallas kernels, scatter_grads(): pl.pallas_call(functools.partial(scatter_kernel, share_rows=share_rows),...  124 us
    dot_general x10, matrix products, scoped(): return jnp.einsum(spec, lhs, rhs, **kwargs)  88.3 us
    pallas_call x2, Pallas kernels, mlp_grad(): pl.pallas_call(functools.partial(mlp_grad_kernel, row1=row1, row2=row2),...  88 us
    pallas_call x1, Pallas kernels, gather_shares(): pl.pallas_call(gather_kernel, out_shape=(jax.ShapeDtypeStruct(flat, dtype...  55 us
    reduce_sum x7, other arithmetic, layer_norm(): normed * ln_gain.astype(jnp.float32) + ln_shift.astype(jnp.float32)  27.3 us
    dot_general x2, matrix products, layer_backward(): jnp.einsum('bsc,js->bcj', d_after_bf, w_tok2, preferred_element_type=jnp....  17.9 us
    dot_general x2, matrix products, layer_forward(): jnp.einsum('bsd,dc->bsc', act_ch, w_ch2, preferred_element_type=jnp.float32)  15.7 us
    reduce_sum x9, other arithmetic, layer_norm(): var_val = jnp.mean(jnp.square(x_f - mean_val), axis=-1, keepdims=True)  14.8 us

profile of v3, /device:TPU:0, one launch (start us, length us, event | category | flops | bytes accessed | tf_op | source)
XLA Modules:
  0.0 540.2 jit_solution(9655826632926091098)
XLA Ops:
  7.9 55.0 %gather_shares.1 = (bf16[8,269,8,128]{3,2,1,0:T(8,128)(2,1)}, bf16[8,269,8,128]{3,2,1,0:T(8,128)(2,1)}, bf16[32,17,8,128]{3,2,1,0:T(8,128)(2,1)}) custom-call(bf16[66,8,128]{2,1,0:T(8,128)(2,1)} %slice_bitcast_fusion.2.inner0_ref, bf16[66,8,128]{2,1,0:T(8,128)(2,1)} %slice_bitcast_fusion.1.inner1_ref, bf16[21,8,128]{2,1,0:T(8,128)(2,1)} %copy-done.44), custom_call_target="tpu_custom_call" | custom-call | tf_op jit(solution)/shard_map/gather_shares/pallas_call | solution.py:215
  67.5 3.7 copy.26
  75.1 5.8 %fusion.95 = f32[16,512,256]{2,1,0:T(8,128)} fusion(f32[512]{0:T(512)} %get-tuple-element.100, f32[512]{0:T(512)} %get-tuple-element.101, f32[16,200]{1,0:T(8,128)S(1)} %add_rsqrt_fusion, f32[16,200]{1,0:T(8,128)S(1)} %broadcast_multiply_fusion.4, bf16[16,196,512]{2,1,0:T(8,128)(2,1)S(1)} %copy.26, bf16[196,256]{1,0:T(8,128)(2,1)} %reshape.390), kind=kOutput, calls=%fused_computation.148 | convolution fusion | flops 848691200 | bytes 11729920 | tf_op jit(solution)/shard_map/f0_tok1/bsc,sj->bcj/dot_general | solution.py:546
  81.5 6.9 %convert_reduce_fusion.3 = (f32[16,200]{1,0:T(8,128)S(1)}, bf16[16,200,512]{2,1,0:T(8,128)(2,1)S(1)}) fusion(f32[200]{0:T(256)S(1)} %copy-done.72, f32[16,512,256]{2,1,0:T(8,128)} %fusion.95, f32[256]{0:T(256)S(1)} %slice_convert_fusion.15, bf16[256,196]{0,1:T(8,128)(2,1)S(1)} %copy.27, bf16[16,196,512]{2,1,0:T(8,128)(2,1)} %copy-done.9), kind=kOutput, calls=%fused_computation.29 | convolution fusion | flops 867562368 | bytes 14991648 | tf_op jit(solution)/shard_map/f0_tok2/bcj,js->bsc/dot_general | solution.py:555
  93.9 5.3 unpack_mats.2
  99.2 23.3 %multiply_add_fusion = (f32[16,200,2048]{2,1,0:T(8,128)}, bf16[16,200,2048]{2,1,0:T(8,128)(2,1)S(1)}) fusion(f32[2048]{0:T(1024)S(1)} %slice_convert_fusion.1, bf16[16,200,512]{2,1,0:T(8,128)(2,1)} %fusion.49, bf16[512,2048]{1,0:T(8,128)(2,1)} %get-tuple-element.28.w1_ref), kind=kOutput, calls=%fused_computation | convolution fusion | flops 6822297600 | bytes 44703744 | tf_op jit(solution)/shard_map/f0_ch1/bsc,cd->bsd/dot_general | solution.py:546
  122.6 7.8 %convert_reduce_fusion.2 = (f32[16,200]{1,0:T(8,128)S(1)}, bf16[16,200,512]{2,1,0:T(8,128)(2,1)S(1)}) fusion(f32[512]{0:T(512)S(1)} %copy-done.60, bf16[16,200,2048]{2,1,0:T(8,128)(2,1)S(1)} %get-tuple-element.83, bf16[2048,512]{1,0:T(8,128)(2,1)S(1)} %copy-done.65, bf16[16,200,512]{2,1,0:T(8,128)(2,1)S(1)} %get-tuple-element.103), kind=kOutput, calls=%fused_computation.22 | convolution fusion | flops 6720713728 | bytes 21772800 | tf_op jit(solution)/shard_map/f0_ch2/bsd,dc->bsc/dot_general | solution.py:561
  135.1 8.0 %fusion.92 = f32[16,512,256]{2,1,0:T(8,128)} fusion(bf16[16,200,512]{2,1,0:T(8,128)(2,1)} %copy-done.5, f32[512]{0:T(512)S(1)} %copy-done.56, f32[512]{0:T(512)S(1)} %get-tuple-element.96, f32[16,200]{1,0:T(8,128)S(1)} %fusion.136, f32[16,200]{1,0:T(8,128)S(1)} %broadcast_multiply_fusion.2, bf16[196,256]{1,0:T(8,128)(2,1)S(1)} %reshape.386), kind=kOutput, calls=%fused_computation.147 | convolution fusion | flops 848691200 | bytes 11795456 | tf_op jit(solution)/shard_map/f1_tok1/bsc,sj->bcj/dot_general | solution.py:546
  144.8 7.4 %convert_reduce_fusion.1 = (f32[16,200]{1,0:T(8,128)S(1)}, bf16[16,200,512]{2,1,0:T(8,128)(2,1)S(1)}) fusion(f32[200]{0:T(256)} %pad_convert_fusion.1, f32[16,512,256]{2,1,0:T(8,128)} %fusion.92, f32[256]{0:T(256)} %slice_convert_fusion.14, bf16[256,196]{0,1:T(8,128)(2,1)S(1)} %copy.28, bf16[16,200,512]{2,1,0:T(8,128)(2,1)S(1)} %copy-done.6), kind=kOutput, calls=%fused_computation.15 | convolution fusion | flops 867562368 | bytes 15057184 | tf_op jit(solution)/shard_map/f1_tok2/bcj,js->bsc/dot_general | solution.py:555
  155.3 5.8 %unpack_mats.3 = (bf16[512,2048]{1,0:T(8,128)(2,1)}, bf16[2048,512]{1,0:T(8,128)(2,1)}) custom-call(bf16[2152,8,128]{2,1,0:T(8,128)(2,1)} %bitcast.216), custom_call_target="tpu_custom_call" | custom-call | bytes 8388608 | tf_op jit(solution)/shard_map/unpack_mats/pallas_call | solution.py:506
  161.1 24.4 %multiply_add_fusion.1 = (f32[16,200,2048]{2,1,0:T(8,128)}, bf16[16,200,2048]{2,1,0:T(8,128)(2,1)S(1)}) fusion(f32[2048]{0:T(1024)S(1)} %copy-done.51, bf16[16,200,512]{2,1,0:T(8,128)(2,1)S(1)} %fusion.42, bf16[512,2048]{1,0:T(8,128)(2,1)} %get-tuple-element.30.w1_ref), kind=kOutput, calls=%fused_computation.1 | convolution fusion | flops 6822297600 | bytes 44703744 | tf_op jit(solution)/shard_map/f1_ch1/bsc,cd->bsd/dot_general | solution.py:546
  185.6 7.8 %convert_reduce_fusion.8 = (f32[16,200]{1,0:T(8,128)S(1)}, bf16[16,200,512]{2,1,0:T(8,128)(2,1)S(1)}) fusion(f32[512]{0:T(512)S(1)} %copy-done.59, bf16[16,200,2048]{2,1,0:T(8,128)(2,1)S(1)} %get-tuple-element.85, bf16[2048,512]{1,0:T(8,128)(2,1)S(1)} %copy-done.66, bf16[16,200,512]{2,1,0:T(8,128)(2,1)S(1)} %copy-done.1), kind=kOutput, calls=%fused_computation.56 | convolution fusion | flops 6720713728 | bytes 21772800 | tf_op jit(solution)/shard_map/f1_ch2/bsd,dc->bsc/dot_general | solution.py:561
  198.4 4.5 fusion.72
  204.8 4.0 fusion.57
  208.7 43.8 %mlp_grad.2 = (bf16[3200,512]{1,0:T(8,128)(2,1)}, f32[8,2048]{1,0:T(8,128)}, f32[17216,128]{1,0:T(8,128)}) custom-call(bf16[3200,512]{1,0:T(8,128)(2,1)} %bitcast.221, bf16[3200,2048]{1,0:T(8,128)(2,1)} %bitcast.249, f32[3200,2048]{1,0:T(8,128)} %bitcast.247, bf16[3200,512]{1,0:T(8,128)(2,1)} %bitcast.223, bf16[512,2048]{1,0:T(8,128)(2,1)} %get-tuple-element.30.w1_ref, ...), custom_call_target="tpu_custom_call" | custom-call | flops 26843545600 | bytes 61734912 | tf_op jit(solution)/shard_map/mlp_grad/pallas_call | solution.py:458
  252.7 4.6 convert_reduce_fusion.11
  257.9 5.3 fusion.43
  265.0 6.2 %convert_reduce_fusion.7 = (f32[512]{0:T(512)}, f32[200]{0:T(256)}, bf16[16,200,512]{2,1,0:T(8,128)(2,1)S(1)}) fusion(f32[16,200]{1,0:T(8,128)S(1)} %add_multiply_fusion.4, f32[16,200]{1,0:T(8,128)S(1)} %multiply_multiply_fusion.4, f32[16,200]{1,0:T(8,128)S(1)} %broadcast_multiply_fusion.1, bf16[16,200,512]{2,1,0:T(8,128)(2,1)S(1)} %copy-done.2, ...), kind=kLoop, calls=%fused_computation.53 | loop fusion | flops 37682488 | bytes 16509928 | tf_op jit(solution)/shard_map/reduce_sum | solution.py:571
  271.2 7.0 %fusion.169 = (f32[256]{0:T(256)}, bf16[16,512,256]{2,1,0:T(8,128)(2,1)S(1)}) fusion(f32[16,512,256]{2,1,0:T(8,128)S(1)} %bitcast.251, f32[256]{0:T(256)S(1)} %copy-done.69, bf16[256,196]{0,1:T(8,128)(2,1)S(1)} %copy-done.31, bf16[16,200,512]{2,1,0:T(8,128)(2,1)S(1)} %copy-done.13, bf16[16,200,512]{2,1,0:T(8,128)(2,1)S(1)} %get-tuple-element.76), kind=kOutput, calls=%fused_computation.294 | convolution fusion | flops 887357184 | bytes 19238912 | tf_op jit(solution)/shard_map/b1_dtok/bsc,js->bcj/dot_general | solution.py:587
  278.2 4.5 fusion.61
  284.4 6.5 %fusion.164 = (bf16[16,200,512]{2,1,0:T(8,128)(2,1)}, f32[16,200,512]{2,1,0:T(8,128)}) fusion(bf16[16,200,512]{2,1,0:T(8,128)(2,1)S(1)} %get-tuple-element.76, f32[16,200]{1,0:T(8,128)S(1)} %add_multiply_fusion.3, f32[16,200]{1,0:T(8,128)S(1)} %multiply_multiply_fusion.3, f32[16,200]{1,0:T(8,128)S(1)} %broadcast_multiply_fusion.2, ...), kind=kLoop, calls=%fused_computation.289 | loop fusion | flops 40960000 | bytes 23060680 | tf_op jit(solution)/shard_map/convert_element_type | solution.py:570
  290.9 44.1 %mlp_grad.3 = (bf16[3200,512]{1,0:T(8,128)(2,1)}, f32[8,2048]{1,0:T(8,128)}, f32[17216,128]{1,0:T(8,128)}) custom-call(bf16[3200,512]{1,0:T(8,128)(2,1)} %bitcast.220, bf16[3200,2048]{1,0:T(8,128)(2,1)} %bitcast.248, f32[3200,2048]{1,0:T(8,128)} %bitcast.246, bf16[3200,512]{1,0:T(8,128)(2,1)} %bitcast.222, bf16[512,2048]{1,0:T(8,128)(2,1)} %get-tuple-element.28.w1_ref, ...), custom_call_target="tpu_custom_call" | custom-call | flops 26843545600 | bytes 61734912 | tf_op jit(solution)/shard_map/mlp_grad/pallas_call | solution.py:458
  335.1 4.0 convert_reduce_fusion.10
  339.3 6.1 %fusion.50 = (f32[512]{0:T(512)S(1)}, f32[16,200]{1,0:T(8,128)S(1)}, f32[16,200,512]{2,1,0:T(8,128)S(1)}) fusion(bf16[16,200,512]{2,1,0:T(8,128)(2,1)S(1)} %copy-done.4, f32[16,200]{1,0:T(8,128)S(1)} %copy-done.23, f32[16,200]{1,0:T(8,128)S(1)} %copy-done.19, f32[512]{0:T(512)S(1)} %copy-done.43, bf16[16,200,512]{2,1,0:T(8,128)(2,1)} %bitcast.207), kind=kLoop, calls=%fused_computation.93 | loop fusion | flops 14741888 | bytes 13149696 | tf_op jit(solution)/shard_map/b0_ln2/transpose(jvp())/reduce_sum | solution.py:526
  347.2 3.9 fusion.157
  351.0 3.2 convolution_bitcast_fusion
  354.6 10.9 %fusion.168 = (f32[256]{0:T(256)}, bf16[16,512,256]{2,1,0:T(8,128)(2,1)S(1)}) fusion(f32[16,512,256]{2,1,0:T(8,128)} %fusion.95, f32[256]{0:T(256)} %copy-done.70, bf16[256,196]{0,1:T(8,128)(2,1)} %copy-done.29, f32[16,200,512]{2,1,0:T(8,128)} %get-tuple-element.80, bf16[16,200,512]{2,1,0:T(8,128)(2,1)} %copy-done.15), kind=kOutput, calls=%fused_computation.293 | convolution fusion | flops 885718784 | bytes 22515712 | tf_op jit(solution)/shard_map/b0_dtok/bsc,js->bcj/dot_general | solution.py:587
  371.3 3.6 fusion.55
  376.1 8.6 %fusion.100 = f32[256,200]{0,1:T(8,128)S(1)} fusion(bf16[16,200,512]{2,1,0:T(8,128)(2,1)} %fusion.57, bf16[16,200,512]{2,1,0:T(8,128)(2,1)} %copy-done.11, f32[16,512,256]{2,1,0:T(8,128)} %fusion.92, f32[256]{0:T(256)} %slice_convert_fusion.14), kind=kOutput, calls=%fused_computation.150 | convolution fusion | flops 864288768 | bytes 15148032 | tf_op jit(solution)/shard_map/b1_gt2/bcj,bsc->js/dot_general | solution.py:546
  386.8 4.5 fusion.103
  403.4 123.5 %scatter_grads.1 = (f32[68,8,128]{2,1,0:T(8,128)}, f32[85,8,128]{2,1,0:T(8,128)}, f32[2,8,128]{2,1,0:T(8,128)}) custom-call(f32[8,269,8,128]{3,2,1,0:T(8,128)} %bitcast.212, f32[8,269,8,128]{3,2,1,0:T(8,128)} %bitcast.211, f32[32,17,8,128]{3,2,1,0:T(8,128)} %select_maximum_fusion.extra_ref, f32[8,128]{1,0:T(8,128)} %pad.74.loss_ref), custom_call_target="tpu_custom_call" | custom-call | tf_op jit(solution)/shard_map/scatter_grads/pallas_call | solution.py:377
  532.4 3.4 multiply_subtract_fusion
  (284 shorter events, 71.9 us)
Async XLA Ops:
  66.9 23.7 %copy-start.42 = (f32[512]{0:T(512)}, f32[512]{0:T(512)S(1)}, u32[]{:S(2)}) copy-start(f32[512]{0:T(512)S(1)} %get-tuple-element.97) | copy-start | bytes 6148
  88.4 34.1 %copy-start.3 = (bf16[16,200,512]{2,1,0:T(8,128)(2,1)}, bf16[16,200,512]{2,1,0:T(8,128)(2,1)S(1)}, u32[]{:S(2)}) copy-start(bf16[16,200,512]{2,1,0:T(8,128)(2,1)S(1)} %get-tuple-element.103) | copy-start | bytes 9830404
  99.2 23.4 %copy-start.60 = (f32[512]{0:T(512)S(1)}, f32[512]{0:T(512)}, u32[]{:S(2)}) copy-start(f32[512]{0:T(512)} %get-tuple-element.98) | copy-start | bytes 6148
  99.2 23.4 %copy-start.65 = (bf16[2048,512]{1,0:T(8,128)(2,1)S(1)}, bf16[2048,512]{1,0:T(8,128)(2,1)}, u32[]{:S(2)}) copy-start(bf16[2048,512]{1,0:T(8,128)(2,1)} %get-tuple-element.29.w2_ref) | copy-start | bytes 6291460
  122.6 12.5 %copy-start.56 = (f32[512]{0:T(512)S(1)}, f32[512]{0:T(512)}, u32[]{:S(2)}) copy-start(f32[512]{0:T(512)} %get-tuple-element.95) | copy-start | bytes 6148
  132.1 152.2 %copy-start.25 = (f32[16,200]{1,0:T(8,128)}, f32[16,200]{1,0:T(8,128)S(1)}, u32[]{:S(2)}) copy-start(f32[16,200]{1,0:T(8,128)S(1)} %broadcast_multiply_fusion.2) | copy-start | bytes 38404
  155.3 30.3 %copy-start.14 = (bf16[16,200,512]{2,1,0:T(8,128)(2,1)}, bf16[16,200,512]{2,1,0:T(8,128)(2,1)S(1)}, u32[]{:S(2)}) copy-start(bf16[16,200,512]{2,1,0:T(8,128)(2,1)S(1)} %fusion.42) | copy-start | bytes 9830404
  161.1 24.5 %copy-start.1 = (bf16[16,200,512]{2,1,0:T(8,128)(2,1)S(1)}, bf16[16,200,512]{2,1,0:T(8,128)(2,1)}, u32[]{:S(2)}) copy-start(bf16[16,200,512]{2,1,0:T(8,128)(2,1)} %copy-done) | copy-start | bytes 9830404
  161.1 24.5 %copy-start.59 = (f32[512]{0:T(512)S(1)}, f32[512]{0:T(512)}, u32[]{:S(2)}) copy-start(f32[512]{0:T(512)} %get-tuple-element.93) | copy-start | bytes 6148
  161.1 24.5 %copy-start.66 = (bf16[2048,512]{1,0:T(8,128)(2,1)S(1)}, bf16[2048,512]{1,0:T(8,128)(2,1)}, u32[]{:S(2)}) copy-start(bf16[2048,512]{1,0:T(8,128)(2,1)} %get-tuple-element.31.w2_ref) | copy-start | bytes 6291460
  257.9 13.2 %slice-start.2 = ((s8[8388608]{0:T(1024)(128)(4,1)}), s8[4194304]{0:T(1024)(128)(4,1)S(1)}, s32[]{:S(2)}) async-start(s8[8388608]{0:T(1024)(128)(4,1)} %bitcast.250), calls=%async_computation.2 | async-start | bytes 8388608
  271.1 13.2 %copy-start.11 = (bf16[16,200,512]{2,1,0:T(8,128)(2,1)}, bf16[16,200,512]{2,1,0:T(8,128)(2,1)S(1)}, u32[]{:S(2)}) copy-start(bf16[16,200,512]{2,1,0:T(8,128)(2,1)S(1)} %get-tuple-element.76) | copy-start | bytes 9830404
  290.8 44.2 %copy-start.23 = (f32[16,200]{1,0:T(8,128)S(1)}, f32[16,200]{1,0:T(8,128)}, u32[]{:S(2)}) copy-start(f32[16,200]{1,0:T(8,128)} %copy-done.22) | copy-start | bytes 38404
  290.9 44.3 %copy-start.43 = (f32[512]{0:T(512)S(1)}, f32[512]{0:T(512)}, u32[]{:S(2)}) copy-start(f32[512]{0:T(512)} %copy-done.42) | copy-start | bytes 6148
  290.9 48.4 %copy-start.4 = (bf16[16,200,512]{2,1,0:T(8,128)(2,1)S(1)}, bf16[16,200,512]{2,1,0:T(8,128)(2,1)}, u32[]{:S(2)}) copy-start(bf16[16,200,512]{2,1,0:T(8,128)(2,1)} %copy-done.3) | copy-start | bytes 9830404
  290.9 48.4 %copy-start.19 = (f32[16,200]{1,0:T(8,128)S(1)}, f32[16,200]{1,0:T(8,128)}, u32[]{:S(2)}) copy-start(f32[16,200]{1,0:T(8,128)} %copy-done.18) | copy-start | bytes 38404
  339.3 11.8 %slice-start.4 = ((s8[8388608]{0:T(1024)(128)(4,1)}), s8[4194304]{0:T(1024)(128)(4,1)S(1)}, s32[]{:S(2)}) async-start(s8[8388608]{0:T(1024)(128)(4,1)} %bitcast.252), calls=%async_computation.4 | async-start | bytes 8388608
  354.6 11.0 %copy-start.10 = (bf16[16,196,512]{2,1,0:T(8,128)(2,1)S(1)}, bf16[16,196,512]{2,1,0:T(8,128)(2,1)}, u32[]{:S(2)}) copy-start(bf16[16,196,512]{2,1,0:T(8,128)(2,1)} %copy-done.9) | copy-start | bytes 9633796
  354.6 10.9 %copy-start.35 = (f32[16,200]{1,0:T(8,128)S(1)}, f32[16,200]{1,0:T(8,128)}, u32[]{:S(2)}) copy-start(f32[16,200]{1,0:T(8,128)} %copy-done.34) | copy-start | bytes 38404
  354.6 10.9 %copy-start.47 = (f32[16,200]{1,0:T(8,128)S(1)}, f32[16,200]{1,0:T(8,128)}, u32[]{:S(2)}) copy-start(f32[16,200]{1,0:T(8,128)} %copy-done.46) | copy-start | bytes 38404
  354.6 10.9 %copy-start.57 = (f32[512]{0:T(512)S(1)}, f32[512]{0:T(512)}, u32[]{:S(2)}) copy-start(f32[512]{0:T(512)} %get-tuple-element.100) | copy-start | bytes 6148
  354.6 10.9 %copy-start.58 = (f32[512]{0:T(512)S(1)}, f32[512]{0:T(512)}, u32[]{:S(2)}) copy-start(f32[512]{0:T(512)} %get-tuple-element.101) | copy-start | bytes 6148
  376.1 10.7 %copy-start.8 = (bf16[16,200,512]{2,1,0:T(8,128)(2,1)S(1)}, bf16[16,200,512]{2,1,0:T(8,128)(2,1)}, u32[]{:S(2)}) copy-start(bf16[16,200,512]{2,1,0:T(8,128)(2,1)} %copy-done.5) | copy-start | bytes 9830404
  386.8 11.9 %copy-start.48 = (f32[512]{0:T(512)S(1)}, f32[512]{0:T(512)}, u32[]{:S(2)}) copy-start(f32[512]{0:T(512)} %get-tuple-element.50) | copy-start | bytes 6148
  386.8 11.9 %copy-start.49 = (f32[512]{0:T(512)S(1)}, f32[512]{0:T(512)}, u32[]{:S(2)}) copy-start(f32[512]{0:T(512)} %get-tuple-element.64) | copy-start | bytes 6148
  391.4 10.2 %copy-start.54 = (f32[16]{0:T(128)S(1)}, f32[16]{0:T(128)}, u32[]{:S(2)}) copy-start(f32[16]{0:T(128)} %copy-done.53) | copy-start | bytes 196
  403.4 129.0 %copy-start.16 = (f32[2,68864]{1,0:T(2,128)S(1)}, f32[2,68864]{1,0:T(2,128)}, u32[]{:S(2)}) copy-start(f32[2,68864]{1,0:T(2,128)} %param.13) | copy-start | bytes 1652740
  403.4 129.0 %copy-start.20 = (f32[2,68864]{1,0:T(2,128)S(1)}, f32[2,68864]{1,0:T(2,128)}, u32[]{:S(2)}) copy-start(f32[2,68864]{1,0:T(2,128)} %param.16) | copy-start | bytes 1652740
  403.4 129.0 %copy-start.21 = (f32[2,68864]{1,0:T(2,128)S(1)}, f32[2,68864]{1,0:T(2,128)}, u32[]{:S(2)}) copy-start(f32[2,68864]{1,0:T(2,128)} %param.19) | copy-start | bytes 1652740
  527.0 10.4 %copy-start.62 = (f32[128]{0:T(128)S(1)}, f32[128]{0:T(128)}, u32[]{:S(2)}) copy-start(f32[128]{0:T(128)} %param.15) | copy-start | bytes 1540
  527.0 10.4 %copy-start.63 = (f32[128]{0:T(128)S(1)}, f32[128]{0:T(128)}, u32[]{:S(2)}) copy-start(f32[128]{0:T(128)} %param.18) | copy-start | bytes 1540
  527.0 10.4 %copy-start.64 = (f32[128]{0:T(128)S(1)}, f32[128]{0:T(128)}, u32[]{:S(2)}) copy-start(f32[128]{0:T(128)} %param.21) | copy-start | bytes 1540
  (49 other events, 281.5 us)

commit v4 on v3

--- a/solution.py
+++ b/solution.py
@@ -574,7 +574,7 @@
     row1 = mat_tiles[0] + mat_tiles[1]
     d_normed2, bias_rows, flat_grad = mlp_grad(
         d_out_bf.reshape(tokens, num_chans), act_ch.reshape(tokens, -1), slope_ch.reshape(tokens, -1), normed2.reshape(tokens, num_chans),
-        w_ch1, w_ch2, flat_len // LANES, row1, row1 + mat_tiles[2], tokens // 5)
+        w_ch1, w_ch2, flat_len // LANES, row1, row1 + mat_tiles[2], tokens // 4)
     g_b_ch1 = jnp.sum(bias_rows, axis=0)
     d_normed2 = d_normed2.reshape(d_out.shape)
     with jax.named_scope(tag + '_ln2'):

time: 550 us -> 553 us (level)
  no operation moved by 1% of the time
where the time goes in v4:
time: 553 us; the launch traced here: 543 us
  Pallas kernels  281 us (51%)
  matrix products  138 us (25%)
  other arithmetic  90.5 us (16%)
  local copies, waits for them, and re-layouts  29.4 us (5%)
    pallas_call x1, Pallas kernels, scatter_grads(): pl.pallas_call(functools.partial(scatter_kernel, share_rows=share_rows),...  123 us
    pallas_call x2, Pallas kernels, mlp_grad(): pl.pallas_call(functools.partial(mlp_grad_kernel, row1=row1, row2=row2),...  91.2 us
    dot_general x10, matrix products, scoped(): return jnp.einsum(spec, lhs, rhs, **kwargs)  88.5 us
    pallas_call x1, Pallas kernels, gather_shares(): pl.pallas_call(gather_kernel, out_shape=(jax.ShapeDtypeStruct(flat, dtype...  55 us
    reduce_sum x7, other arithmetic, layer_norm(): normed * ln_gain.astype(jnp.float32) + ln_shift.astype(jnp.float32)  27.5 us
    dot_general x2, matrix products, layer_backward(): jnp.einsum('bsc,js->bcj', d_after_bf, w_tok2, preferred_element_type=jnp....  17.6 us
    dot_general x2, matrix products, layer_forward(): jnp.einsum('bsd,dc->bsc', act_ch, w_ch2, preferred_element_type=jnp.float32)  15.7 us
    reduce_sum x9, other arithmetic, layer_norm(): var_val = jnp.mean(jnp.square(x_f - mean_val), axis=-1, keepdims=True)  14.9 us

profile of v4, /device:TPU:0, one launch (start us, length us, event | category | flops | bytes accessed | tf_op | source)
XLA Modules:
  0.0 543.4 jit_solution(15791157840250138429)
XLA Ops:
  7.9 55.0 %gather_shares.1 = (bf16[8,269,8,128]{3,2,1,0:T(8,128)(2,1)}, bf16[8,269,8,128]{3,2,1,0:T(8,128)(2,1)}, bf16[32,17,8,128]{3,2,1,0:T(8,128)(2,1)}) custom-call(bf16[66,8,128]{2,1,0:T(8,128)(2,1)} %slice_bitcast_fusion.2.inner0_ref, bf16[66,8,128]{2,1,0:T(8,128)(2,1)} %slice_bitcast_fusion.1.inner1_ref, bf16[21,8,128]{2,1,0:T(8,128)(2,1)} %copy-done.44), custom_call_target="tpu_custom_call" | custom-call | tf_op jit(solution)/shard_map/gather_shares/pallas_call | solution.py:215
  67.5 3.7 copy.26
  75.1 5.8 %fusion.95 = f32[16,512,256]{2,1,0:T(8,128)} fusion(f32[512]{0:T(512)} %get-tuple-element.100, f32[512]{0:T(512)} %get-tuple-element.101, f32[16,200]{1,0:T(8,128)S(1)} %add_rsqrt_fusion, f32[16,200]{1,0:T(8,128)S(1)} %broadcast_multiply_fusion.4, bf16[16,196,512]{2,1,0:T(8,128)(2,1)S(1)} %copy.26, bf16[196,256]{1,0:T(8,128)(2,1)} %reshape.390), kind=kOutput, calls=%fused_computation.148 | convolution fusion | flops 848691200 | bytes 11729920 | tf_op jit(solution)/shard_map/f0_tok1/bsc,sj->bcj/dot_general | solution.py:546
  81.5 6.9 %convert_reduce_fusion.3 = (f32[16,200]{1,0:T(8,128)S(1)}, bf16[16,200,512]{2,1,0:T(8,128)(2,1)S(1)}) fusion(f32[200]{0:T(256)S(1)} %copy-done.72, f32[16,512,256]{2,1,0:T(8,128)} %fusion.95, f32[256]{0:T(256)S(1)} %slice_convert_fusion.15, bf16[256,196]{0,1:T(8,128)(2,1)S(1)} %copy.27, bf16[16,196,512]{2,1,0:T(8,128)(2,1)} %copy-done.9), kind=kOutput, calls=%fused_computation.29 | convolution fusion | flops 867562368 | bytes 14991648 | tf_op jit(solution)/shard_map/f0_tok2/bcj,js->bsc/dot_general | solution.py:555
  94.2 5.3 unpack_mats.2
  99.5 23.3 %multiply_add_fusion = (f32[16,200,2048]{2,1,0:T(8,128)}, bf16[16,200,2048]{2,1,0:T(8,128)(2,1)S(1)}) fusion(f32[2048]{0:T(1024)S(1)} %slice_convert_fusion.1, bf16[16,200,512]{2,1,0:T(8,128)(2,1)} %fusion.49, bf16[512,2048]{1,0:T(8,128)(2,1)} %get-tuple-element.28.w1_ref), kind=kOutput, calls=%fused_computation | convolution fusion | flops 6822297600 | bytes 44703744 | tf_op jit(solution)/shard_map/f0_ch1/bsc,cd->bsd/dot_general | solution.py:546
  122.8 7.8 %convert_reduce_fusion.2 = (f32[16,200]{1,0:T(8,128)S(1)}, bf16[16,200,512]{2,1,0:T(8,128)(2,1)S(1)}) fusion(f32[512]{0:T(512)S(1)} %copy-done.60, bf16[16,200,2048]{2,1,0:T(8,128)(2,1)S(1)} %get-tuple-element.83, bf16[2048,512]{1,0:T(8,128)(2,1)S(1)} %copy-done.65, bf16[16,200,512]{2,1,0:T(8,128)(2,1)S(1)} %get-tuple-element.103), kind=kOutput, calls=%fused_computation.22 | convolution fusion | flops 6720713728 | bytes 21772800 | tf_op jit(solution)/shard_map/f0_ch2/bsd,dc->bsc/dot_general | solution.py:561
  135.1 8.0 %fusion.92 = f32[16,512,256]{2,1,0:T(8,128)} fusion(bf16[16,200,512]{2,1,0:T(8,128)(2,1)} %copy-done.5, f32[512]{0:T(512)S(1)} %copy-done.56, f32[512]{0:T(512)S(1)} %get-tuple-element.96, f32[16,200]{1,0:T(8,128)S(1)} %fusion.136, f32[16,200]{1,0:T(8,128)S(1)} %broadcast_multiply_fusion.2, bf16[196,256]{1,0:T(8,128)(2,1)S(1)} %reshape.386), kind=kOutput, calls=%fused_computation.147 | convolution fusion | flops 848691200 | bytes 11795456 | tf_op jit(solution)/shard_map/f1_tok1/bsc,sj->bcj/dot_general | solution.py:546
  144.8 7.4 %convert_reduce_fusion.1 = (f32[16,200]{1,0:T(8,128)S(1)}, bf16[16,200,512]{2,1,0:T(8,128)(2,1)S(1)}) fusion(f32[200]{0:T(256)} %pad_convert_fusion.1, f32[16,512,256]{2,1,0:T(8,128)} %fusion.92, f32[256]{0:T(256)} %slice_convert_fusion.14, bf16[256,196]{0,1:T(8,128)(2,1)S(1)} %copy.28, bf16[16,200,512]{2,1,0:T(8,128)(2,1)S(1)} %copy-done.6), kind=kOutput, calls=%fused_computation.15 | convolution fusion | flops 867562368 | bytes 15057184 | tf_op jit(solution)/shard_map/f1_tok2/bcj,js->bsc/dot_general | solution.py:555
  155.3 5.8 %unpack_mats.3 = (bf16[512,2048]{1,0:T(8,128)(2,1)}, bf16[2048,512]{1,0:T(8,128)(2,1)}) custom-call(bf16[2152,8,128]{2,1,0:T(8,128)(2,1)} %bitcast.216), custom_call_target="tpu_custom_call" | custom-call | bytes 8388608 | tf_op jit(solution)/shard_map/unpack_mats/pallas_call | solution.py:506
  161.1 24.5 %multiply_add_fusion.1 = (f32[16,200,2048]{2,1,0:T(8,128)}, bf16[16,200,2048]{2,1,0:T(8,128)(2,1)S(1)}) fusion(f32[2048]{0:T(1024)S(1)} %copy-done.51, bf16[16,200,512]{2,1,0:T(8,128)(2,1)S(1)} %fusion.42, bf16[512,2048]{1,0:T(8,128)(2,1)} %get-tuple-element.30.w1_ref), kind=kOutput, calls=%fused_computation.1 | convolution fusion | flops 6822297600 | bytes 44703744 | tf_op jit(solution)/shard_map/f1_ch1/bsc,cd->bsd/dot_general | solution.py:546
  185.7 7.8 %convert_reduce_fusion.8 = (f32[16,200]{1,0:T(8,128)S(1)}, bf16[16,200,512]{2,1,0:T(8,128)(2,1)S(1)}) fusion(f32[512]{0:T(512)S(1)} %copy-done.59, bf16[16,200,2048]{2,1,0:T(8,128)(2,1)S(1)} %get-tuple-element.85, bf16[2048,512]{1,0:T(8,128)(2,1)S(1)} %copy-done.66, bf16[16,200,512]{2,1,0:T(8,128)(2,1)S(1)} %copy-done.1), kind=kOutput, calls=%fused_computation.56 | convolution fusion | flops 6720713728 | bytes 21772800 | tf_op jit(solution)/shard_map/f1_ch2/bsd,dc->bsc/dot_general | solution.py:561
  198.4 4.5 fusion.72
  205.0 4.0 fusion.57
  209.0 45.5 %mlp_grad.2 = (bf16[3200,512]{1,0:T(8,128)(2,1)}, f32[8,2048]{1,0:T(8,128)}, f32[17216,128]{1,0:T(8,128)}) custom-call(bf16[3200,512]{1,0:T(8,128)(2,1)} %bitcast.221, bf16[3200,2048]{1,0:T(8,128)(2,1)} %bitcast.249, f32[3200,2048]{1,0:T(8,128)} %bitcast.247, bf16[3200,512]{1,0:T(8,128)(2,1)} %bitcast.223, bf16[512,2048]{1,0:T(8,128)(2,1)} %get-tuple-element.30.w1_ref, ...), custom_call_target="tpu_custom_call" | custom-call | flops 26843545600 | bytes 61734912 | tf_op jit(solution)/shard_map/mlp_grad/pallas_call | solution.py:458
  254.7 4.6 convert_reduce_fusion.11
  259.9 5.5 %fusion.43 = (f32[512]{0:T(512)}, f32[16,200]{1,0:T(8,128)S(1)}, f32[16,200,512]{2,1,0:T(8,128)S(1)}) fusion(bf16[16,200,512]{2,1,0:T(8,128)(2,1)} %copy-done, f32[16,200]{1,0:T(8,128)S(1)} %fusion.137, f32[16,200]{1,0:T(8,128)S(1)} %broadcast_multiply_fusion.1, f32[512]{0:T(512)S(1)} %get-tuple-element.92, bf16[16,200,512]{2,1,0:T(8,128)(2,1)} %bitcast.208), kind=kLoop, calls=%fused_computation.86 | loop fusion | flops 14741888 | bytes 13149696 | tf_op jit(solution)/shard_map/b1_ln2/transpose(jvp())/reduce_sum | solution.py:526
  267.1 5.7 %convert_reduce_fusion.7 = (f32[512]{0:T(512)}, f32[200]{0:T(256)}, bf16[16,200,512]{2,1,0:T(8,128)(2,1)S(1)}) fusion(f32[16,200]{1,0:T(8,128)S(1)} %add_multiply_fusion.4, f32[16,200]{1,0:T(8,128)S(1)} %multiply_multiply_fusion.4, f32[16,200]{1,0:T(8,128)S(1)} %broadcast_multiply_fusion.1, bf16[16,200,512]{2,1,0:T(8,128)(2,1)S(1)} %copy-done.2, ...), kind=kLoop, calls=%fused_computation.53 | loop fusion | flops 37682488 | bytes 16509928 | tf_op jit(solution)/shard_map/reduce_sum | solution.py:571
  273.0 7.0 %fusion.169 = (f32[256]{0:T(256)}, bf16[16,512,256]{2,1,0:T(8,128)(2,1)S(1)}) fusion(f32[16,512,256]{2,1,0:T(8,128)S(1)} %bitcast.251, f32[256]{0:T(256)S(1)} %copy-done.69, bf16[256,196]{0,1:T(8,128)(2,1)S(1)} %copy-done.31, bf16[16,200,512]{2,1,0:T(8,128)(2,1)S(1)} %copy-done.13, bf16[16,200,512]{2,1,0:T(8,128)(2,1)S(1)} %get-tuple-element.76), kind=kOutput, calls=%fused_computation.294 | convolution fusion | flops 887357184 | bytes 19238912 | tf_op jit(solution)/shard_map/b1_dtok/bsc,js->bcj/dot_general | solution.py:587
  279.9 4.5 fusion.61
  286.1 6.5 %fusion.164 = (bf16[16,200,512]{2,1,0:T(8,128)(2,1)}, f32[16,200,512]{2,1,0:T(8,128)}) fusion(bf16[16,200,512]{2,1,0:T(8,128)(2,1)S(1)} %get-tuple-element.76, f32[16,200]{1,0:T(8,128)S(1)} %add_multiply_fusion.3, f32[16,200]{1,0:T(8,128)S(1)} %multiply_multiply_fusion.3, f32[16,200]{1,0:T(8,128)S(1)} %broadcast_multiply_fusion.2, ...), kind=kLoop, calls=%fused_computation.289 | loop fusion | flops 40960000 | bytes 23060680 | tf_op jit(solution)/shard_map/convert_element_type | solution.py:570
  292.6 45.7 %mlp_grad.3 = (bf16[3200,512]{1,0:T(8,128)(2,1)}, f32[8,2048]{1,0:T(8,128)}, f32[17216,128]{1,0:T(8,128)}) custom-call(bf16[3200,512]{1,0:T(8,128)(2,1)} %bitcast.220, bf16[3200,2048]{1,0:T(8,128)(2,1)} %bitcast.248, f32[3200,2048]{1,0:T(8,128)} %bitcast.246, bf16[3200,512]{1,0:T(8,128)(2,1)} %bitcast.222, bf16[512,2048]{1,0:T(8,128)(2,1)} %get-tuple-element.28.w1_ref, ...), custom_call_target="tpu_custom_call" | custom-call | flops 26843545600 | bytes 61734912 | tf_op jit(solution)/shard_map/mlp_grad/pallas_call | solution.py:458
  338.5 4.0 convert_reduce_fusion.10
  342.6 6.1 %fusion.50 = (f32[512]{0:T(512)S(1)}, f32[16,200]{1,0:T(8,128)S(1)}, f32[16,200,512]{2,1,0:T(8,128)S(1)}) fusion(bf16[16,200,512]{2,1,0:T(8,128)(2,1)S(1)} %copy-done.4, f32[16,200]{1,0:T(8,128)S(1)} %copy-done.23, f32[16,200]{1,0:T(8,128)S(1)} %copy-done.19, f32[512]{0:T(512)S(1)} %copy-done.43, bf16[16,200,512]{2,1,0:T(8,128)(2,1)} %bitcast.207), kind=kLoop, calls=%fused_computation.93 | loop fusion | flops 14741888 | bytes 13149696 | tf_op jit(solution)/shard_map/b0_ln2/transpose(jvp())/reduce_sum | solution.py:526
  350.5 4.3 fusion.157
  354.8 3.2 convolution_bitcast_fusion
  358.4 10.7 %fusion.168 = (f32[256]{0:T(256)}, bf16[16,512,256]{2,1,0:T(8,128)(2,1)S(1)}) fusion(f32[16,512,256]{2,1,0:T(8,128)} %fusion.95, f32[256]{0:T(256)} %copy-done.70, bf16[256,196]{0,1:T(8,128)(2,1)} %copy-done.29, f32[16,200,512]{2,1,0:T(8,128)} %get-tuple-element.80, bf16[16,200,512]{2,1,0:T(8,128)(2,1)} %copy-done.15), kind=kOutput, calls=%fused_computation.293 | convolution fusion | flops 885718784 | bytes 22515712 | tf_op jit(solution)/shard_map/b0_dtok/bsc,js->bcj/dot_general | solution.py:587
  374.8 3.6 fusion.55
  379.7 8.8 %fusion.100 = f32[256,200]{0,1:T(8,128)S(1)} fusion(bf16[16,200,512]{2,1,0:T(8,128)(2,1)} %fusion.57, bf16[16,200,512]{2,1,0:T(8,128)(2,1)} %copy-done.11, f32[16,512,256]{2,1,0:T(8,128)} %fusion.92, f32[256]{0:T(256)} %slice_convert_fusion.14), kind=kOutput, calls=%fused_computation.150 | convolution fusion | flops 864288768 | bytes 15148032 | tf_op jit(solution)/shard_map/b1_gt2/bcj,bsc->js/dot_general | solution.py:546
  390.5 4.5 fusion.103
  407.1 123.3 %scatter_grads.1 = (f32[68,8,128]{2,1,0:T(8,128)}, f32[85,8,128]{2,1,0:T(8,128)}, f32[2,8,128]{2,1,0:T(8,128)}) custom-call(f32[8,269,8,128]{3,2,1,0:T(8,128)} %bitcast.212, f32[8,269,8,128]{3,2,1,0:T(8,128)} %bitcast.211, f32[32,17,8,128]{3,2,1,0:T(8,128)} %select_maximum_fusion.extra_ref, f32[8,128]{1,0:T(8,128)} %pad.74.loss_ref), custom_call_target="tpu_custom_call" | custom-call | tf_op jit(solution)/shard_map/scatter_grads/pallas_call | solution.py:377
  535.9 3.4 multiply_subtract_fusion
  (284 shorter events, 72.2 us)
Async XLA Ops:
  66.9 23.7 %copy-start.42 = (f32[512]{0:T(512)}, f32[512]{0:T(512)S(1)}, u32[]{:S(2)}) copy-start(f32[512]{0:T(512)S(1)} %get-tuple-element.97) | copy-start | bytes 6148
  88.4 34.4 %copy-start.3 = (bf16[16,200,512]{2,1,0:T(8,128)(2,1)}, bf16[16,200,512]{2,1,0:T(8,128)(2,1)S(1)}, u32[]{:S(2)}) copy-start(bf16[16,200,512]{2,1,0:T(8,128)(2,1)S(1)} %get-tuple-element.103) | copy-start | bytes 9830404
  99.4 23.4 %copy-start.60 = (f32[512]{0:T(512)S(1)}, f32[512]{0:T(512)}, u32[]{:S(2)}) copy-start(f32[512]{0:T(512)} %get-tuple-element.98) | copy-start | bytes 6148
  99.5 23.4 %copy-start.65 = (bf16[2048,512]{1,0:T(8,128)(2,1)S(1)}, bf16[2048,512]{1,0:T(8,128)(2,1)}, u32[]{:S(2)}) copy-start(bf16[2048,512]{1,0:T(8,128)(2,1)} %get-tuple-element.29.w2_ref) | copy-start | bytes 6291460
  122.8 12.2 %copy-start.56 = (f32[512]{0:T(512)S(1)}, f32[512]{0:T(512)}, u32[]{:S(2)}) copy-start(f32[512]{0:T(512)} %get-tuple-element.95) | copy-start | bytes 6148
  132.4 153.7 %copy-start.25 = (f32[16,200]{1,0:T(8,128)}, f32[16,200]{1,0:T(8,128)S(1)}, u32[]{:S(2)}) copy-start(f32[16,200]{1,0:T(8,128)S(1)} %broadcast_multiply_fusion.2) | copy-start | bytes 38404
  155.3 30.3 %copy-start.14 = (bf16[16,200,512]{2,1,0:T(8,128)(2,1)}, bf16[16,200,512]{2,1,0:T(8,128)(2,1)S(1)}, u32[]{:S(2)}) copy-start(bf16[16,200,512]{2,1,0:T(8,128)(2,1)S(1)} %fusion.42) | copy-start | bytes 9830404
  161.1 24.5 %copy-start.1 = (bf16[16,200,512]{2,1,0:T(8,128)(2,1)S(1)}, bf16[16,200,512]{2,1,0:T(8,128)(2,1)}, u32[]{:S(2)}) copy-start(bf16[16,200,512]{2,1,0:T(8,128)(2,1)} %copy-done) | copy-start | bytes 9830404
  161.1 24.5 %copy-start.59 = (f32[512]{0:T(512)S(1)}, f32[512]{0:T(512)}, u32[]{:S(2)}) copy-start(f32[512]{0:T(512)} %get-tuple-element.93) | copy-start | bytes 6148
  161.1 24.5 %copy-start.66 = (bf16[2048,512]{1,0:T(8,128)(2,1)S(1)}, bf16[2048,512]{1,0:T(8,128)(2,1)}, u32[]{:S(2)}) copy-start(bf16[2048,512]{1,0:T(8,128)(2,1)} %get-tuple-element.31.w2_ref) | copy-start | bytes 6291460
  259.9 13.0 %slice-start.2 = ((s8[8388608]{0:T(1024)(128)(4,1)}), s8[4194304]{0:T(1024)(128)(4,1)S(1)}, s32[]{:S(2)}) async-start(s8[8388608]{0:T(1024)(128)(4,1)} %bitcast.250), calls=%async_computation.2 | async-start | bytes 8388608
  272.9 13.2 %copy-start.11 = (bf16[16,200,512]{2,1,0:T(8,128)(2,1)}, bf16[16,200,512]{2,1,0:T(8,128)(2,1)S(1)}, u32[]{:S(2)}) copy-start(bf16[16,200,512]{2,1,0:T(8,128)(2,1)S(1)} %get-tuple-element.76) | copy-start | bytes 9830404
  292.6 45.7 %copy-start.23 = (f32[16,200]{1,0:T(8,128)S(1)}, f32[16,200]{1,0:T(8,128)}, u32[]{:S(2)}) copy-start(f32[16,200]{1,0:T(8,128)} %copy-done.22) | copy-start | bytes 38404
  292.6 45.8 %copy-start.43 = (f32[512]{0:T(512)S(1)}, f32[512]{0:T(512)}, u32[]{:S(2)}) copy-start(f32[512]{0:T(512)} %copy-done.42) | copy-start | bytes 6148
  292.6 49.9 %copy-start.4 = (bf16[16,200,512]{2,1,0:T(8,128)(2,1)S(1)}, bf16[16,200,512]{2,1,0:T(8,128)(2,1)}, u32[]{:S(2)}) copy-start(bf16[16,200,512]{2,1,0:T(8,128)(2,1)} %copy-done.3) | copy-start | bytes 9830404
  292.6 49.9 %copy-start.19 = (f32[16,200]{1,0:T(8,128)S(1)}, f32[16,200]{1,0:T(8,128)}, u32[]{:S(2)}) copy-start(f32[16,200]{1,0:T(8,128)} %copy-done.18) | copy-start | bytes 38404
  342.6 12.2 %slice-start.4 = ((s8[8388608]{0:T(1024)(128)(4,1)}), s8[4194304]{0:T(1024)(128)(4,1)S(1)}, s32[]{:S(2)}) async-start(s8[8388608]{0:T(1024)(128)(4,1)} %bitcast.252), calls=%async_computation.4 | async-start | bytes 8388608
  358.3 10.7 %copy-start.10 = (bf16[16,196,512]{2,1,0:T(8,128)(2,1)S(1)}, bf16[16,196,512]{2,1,0:T(8,128)(2,1)}, u32[]{:S(2)}) copy-start(bf16[16,196,512]{2,1,0:T(8,128)(2,1)} %copy-done.9) | copy-start | bytes 9633796
  358.3 10.7 %copy-start.35 = (f32[16,200]{1,0:T(8,128)S(1)}, f32[16,200]{1,0:T(8,128)}, u32[]{:S(2)}) copy-start(f32[16,200]{1,0:T(8,128)} %copy-done.34) | copy-start | bytes 38404
  358.3 10.7 %copy-start.47 = (f32[16,200]{1,0:T(8,128)S(1)}, f32[16,200]{1,0:T(8,128)}, u32[]{:S(2)}) copy-start(f32[16,200]{1,0:T(8,128)} %copy-done.46) | copy-start | bytes 38404
  358.3 10.7 %copy-start.57 = (f32[512]{0:T(512)S(1)}, f32[512]{0:T(512)}, u32[]{:S(2)}) copy-start(f32[512]{0:T(512)} %get-tuple-element.100) | copy-start | bytes 6148
  358.4 10.7 %copy-start.58 = (f32[512]{0:T(512)S(1)}, f32[512]{0:T(512)}, u32[]{:S(2)}) copy-start(f32[512]{0:T(512)} %get-tuple-element.101) | copy-start | bytes 6148
  379.6 10.8 %copy-start.8 = (bf16[16,200,512]{2,1,0:T(8,128)(2,1)S(1)}, bf16[16,200,512]{2,1,0:T(8,128)(2,1)}, u32[]{:S(2)}) copy-start(bf16[16,200,512]{2,1,0:T(8,128)(2,1)} %copy-done.5) | copy-start | bytes 9830404
  390.5 11.9 %copy-start.48 = (f32[512]{0:T(512)S(1)}, f32[512]{0:T(512)}, u32[]{:S(2)}) copy-start(f32[512]{0:T(512)} %get-tuple-element.50) | copy-start | bytes 6148
  390.5 11.9 %copy-start.49 = (f32[512]{0:T(512)S(1)}, f32[512]{0:T(512)}, u32[]{:S(2)}) copy-start(f32[512]{0:T(512)} %get-tuple-element.64) | copy-start | bytes 6148
  395.1 10.2 %copy-start.54 = (f32[16]{0:T(128)S(1)}, f32[16]{0:T(128)}, u32[]{:S(2)}) copy-start(f32[16]{0:T(128)} %copy-done.53) | copy-start | bytes 196
  407.1 128.8 %copy-start.16 = (f32[2,68864]{1,0:T(2,128)S(1)}, f32[2,68864]{1,0:T(2,128)}, u32[]{:S(2)}) copy-start(f32[2,68864]{1,0:T(2,128)} %param.13) | copy-start | bytes 1652740
  407.1 128.8 %copy-start.20 = (f32[2,68864]{1,0:T(2,128)S(1)}, f32[2,68864]{1,0:T(2,128)}, u32[]{:S(2)}) copy-start(f32[2,68864]{1,0:T(2,128)} %param.16) | copy-start | bytes 1652740
  407.1 128.8 %copy-start.21 = (f32[2,68864]{1,0:T(2,128)S(1)}, f32[2,68864]{1,0:T(2,128)}, u32[]{:S(2)}) copy-start(f32[2,68864]{1,0:T(2,128)} %param.19) | copy-start | bytes 1652740
  530.5 10.4 %copy-start.62 = (f32[128]{0:T(128)S(1)}, f32[128]{0:T(128)}, u32[]{:S(2)}) copy-start(f32[128]{0:T(128)} %param.15) | copy-start | bytes 1540
  530.5 10.4 %copy-start.63 = (f32[128]{0:T(128)S(1)}, f32[128]{0:T(128)}, u32[]{:S(2)}) copy-start(f32[128]{0:T(128)} %param.18) | copy-start | bytes 1540
  530.5 10.4 %copy-start.64 = (f32[128]{0:T(128)S(1)}, f32[128]{0:T(128)}, u32[]{:S(2)}) copy-start(f32[128]{0:T(128)} %param.21) | copy-start | bytes 1540
  (49 other events, 281.0 us)
